TPU v7x, 32 devices: a whole 2x2x4 slice. The times are simulated.
32 devices in a mesh: pulse: 8 (over z, core), range: 4 (over y, x).
Axes of the slice: x: 2, y: 2, z: 4, core: 2. Of those that a mesh axis runs over, the one named last changes fastest.
Arguments:
- pulse_data: bfloat16 [2, 8192, 4096], P(None, 'pulse', 'range'), may hold values from -6 to 6
- merge_taps: int32 [3, 2, 4, 8192], P(None, None, None, 'pulse'), may hold values from 0 to 1023, as said below
- merge_weights: bfloat16 [3, 2, 4, 8192], P(None, None, None, 'pulse'), may hold values from -2 to 2
- squint: float32 [3, 8192], P(None, 'pulse'), may hold values from -8 to 8
Outputs:
- focused: float32 [2, 1024, 4096], P(None, 'pulse', 'range')
Inputs may be any that keep to these rules, and one draw needn't show every extreme that they name: `merge_taps`: for each level, source half and output beam, the 4 taps name different beams of the source block.
All inputs are finite; a program needn't handle non-finite values.
Results may differ from a plain program's by a relative error of at most 0.0064.
Values may be sent and summed in bfloat16 or wider, within the bound.
No kernel may reach another device: no remote copies, remote signals or barrier semaphores. Data moves between devices by JAX's collectives and lax.ppermute only.
A program may use at most 64 MiB of HBM per device.

v0:
```python
import functools
import math

import jax
import jax.numpy as jnp
from jax import lax
from jax.experimental import pallas as pl
from jax.experimental.pallas import tpu as pltpu
from jax.sharding import PartitionSpec as P


BINS = 1024
BLOCK = 64
POWER = 3
MIB = 1024 * 1024
SMALL_LIMIT = 4
LANES = 128
EPSILON = 1e-06


F32 = jnp.float32
BF16 = jnp.bfloat16


SINE = (3.1415926401307077, -5.16771008350789, 2.550077523214589, -0.5982912856206265, 0.07765766030630428)
COSINE = (0.9999999532476085, -4.934792830619644, 4.058411352862619, -1.3318765680811142, 0.2196896110983216)


def cis_turns(turns):
    z = turns - jnp.floor(turns + 0.5)
    w = z * z
    s, c = SINE[-1], COSINE[-1]
    for more in SINE[-2::-1]:
        s = s * w + more
    for more in COSINE[-2::-1]:
        c = c * w + more
    s = s * z
    twice = s + s
    return 1.0 - twice * s, twice * c


def swap(block, axis, distance):
    count = lax.axis_size(axis)
    return lax.ppermute(block, axis, [(i, i ^ distance) for i in range(count)])


VMEM = pl.BlockSpec(memory_space=pltpu.VMEM)
SMEM = pl.BlockSpec(memory_space=pltpu.SMEM)
HBM = pl.BlockSpec(memory_space=pltpu.HBM)


def pack_kernel(taps, weights, squint, mine, near, far):
    def put(out, row, level, source):
        out[row : row + 4] = taps[level, source].astype(F32)
        out[row + 4 : row + 8] = weights[level, source].astype(F32)

    put(mine, 0, 0, 0)
    put(mine, 8, 0, 1)
    put(mine, 16, 1, 0)
    put(mine, 24, 2, 0)
    mine[32:35] = squint[...]
    mine[35:40] = jnp.zeros((5, mine.shape[1]), F32)
    put(near, 0, 1, 1)
    put(near, 8, 2, 0)
    near[16:19] = squint[...]
    near[19:24] = jnp.zeros((5, near.shape[1]), F32)
    put(far, 0, 2, 1)
    far[8:11] = squint[...]
    far[11:16] = jnp.zeros((5, far.shape[1]), F32)


def pack(taps, weights, squint):
    beams = squint.shape[1]
    return pl.pallas_call(
        pack_kernel,
        in_specs=[VMEM] * 3,
        out_specs=[VMEM] * 3,
        out_shape=[jax.ShapeDtypeStruct((rows, beams), F32) for rows in (40, 24, 16)],
        compiler_params=pltpu.CompilerParams(vmem_limit_bytes=SMALL_LIMIT * MIB),
        name="pack",
    )(taps, weights, squint)


def fill_matrices(columns, outs):
    beams = columns.shape[0]

    def part(i, _):
        at = pl.ds(pl.multiple_of(i * 16, 16), 16)
        lane = lax.broadcasted_iota(jnp.int32, (16, LANES), 1)
        lanes = [(lane + j * LANES).astype(jnp.int16) for j in range(beams // LANES)]
        p = columns[at, :]

        def spread(column):
            return jnp.broadcast_to(p[:, column : column + 1], (16, LANES))

        for unit, out in enumerate(outs):
            taps = [spread(8 * unit + c).astype(jnp.int32).astype(jnp.int16) for c in range(4)]
            weights = [spread(8 * unit + 4 + c).astype(BF16) for c in range(4)]
            for j, here in enumerate(lanes):
                total = jnp.zeros((16, LANES), BF16)
                for tap, weight in zip(taps, weights):
                    total = jnp.where(here == tap, weight, total)
                out[at, j * LANES : (j + 1) * LANES] = total
        return 0

    lax.fori_loop(0, beams // 16, part, 0, unroll=2)


def first_kernel(pulses, scalars, mine, matrices, table, columns, rows):
    beams = matrices.shape[1]
    angles = beams * pulses
    classes = pulses // 2
    each = BINS // pulses
    rows[0:40] = mine[...]
    columns[...] = rows[...].T
    fill_matrices(columns, [matrices.at[u] for u in range(2)])
    count = BINS // classes
    inner = each // classes
    bits = pulses.bit_length() - 1

    def part(i, _):
        at = pl.ds(pl.multiple_of(i * 16, 16), 16)
        row = lax.broadcasted_iota(jnp.int32, (16, LANES), 0) + i * 16
        group = (row & (count - 1)) >> (inner.bit_length() - 1)
        mirrored = jnp.zeros_like(group)
        for bit in range(bits):
            mirrored = mirrored | ((group >> bit & 1) << (bits - 1 - bit))
        bins = (
            (mirrored ^ scalars[0]) * each
            + (row & (inner - 1)) * classes
            + (row >> (count.bit_length() - 1))
        )
        lane = lax.broadcasted_iota(jnp.int32, (16, LANES), 1)
        whole = angles - 1
        fine_c, fine_s = cis_turns((bins * lane & whole).astype(F32) * (1.0 / angles))
        coarse_c, coarse_s = cis_turns(
            (bins * (scalars[2] + lane * LANES & whole) & whole).astype(F32) * (1.0 / angles)
        )
        low = i * 16 + (i * 16 >> (count.bit_length() - 1)) * count
        cos_at = pl.ds(pl.multiple_of(low, 16), 16)
        sin_at = pl.ds(pl.multiple_of(low + count, 16), 16)
        for j in range(beams // LANES):
            a_c = coarse_c[:, j : j + 1]
            a_s = coarse_s[:, j : j + 1]
            lanes = slice(j * LANES, (j + 1) * LANES)
            table[cos_at, lanes] = (a_c * fine_c - a_s * fine_s).astype(BF16)
            table[sin_at, lanes] = (a_s * fine_c + a_c * fine_s).astype(BF16)
        return 0

    lax.fori_loop(0, BINS // 16, part, 0, unroll=2)


def first_tables(scalars, mine, pulses):
    beams = mine.shape[1]
    return pl.pallas_call(
        functools.partial(first_kernel, pulses),
        in_specs=[SMEM, VMEM],
        out_specs=[VMEM] * 2,
        out_shape=[
            jax.ShapeDtypeStruct((2, beams, beams), BF16),
            jax.ShapeDtypeStruct((2 * BINS, beams), BF16),
        ],
        scratch_shapes=[pltpu.VMEM((beams, LANES), F32), pltpu.VMEM((LANES, beams), F32)],
        compiler_params=pltpu.CompilerParams(vmem_limit_bytes=SMALL_LIMIT * MIB),
        cost_estimate=pl.CostEstimate(
            flops=30 * beams * beams, bytes_accessed=8 * beams * beams, transcendentals=0
        ),
        name="first",
    )(scalars, mine)


def fetch(pulse_data, other, here, there, sems, start):
    return [
        pltpu.make_async_copy(
            source.at[t, :, pl.ds(start + j * LANES, LANES)],
            to.at[j, :, pl.ds(t * LANES, LANES)],
            sems.at[i, j, t],
        )
        for i, (source, to) in enumerate(((pulse_data, here), (other, there)))
        for j in range(here.shape[0])
        for t in range(2)
    ]


def second_kernel(
    ranges,
    scalars, mine, near, middle, far, pulse_data, other,
    split, join, phase, step, here, there,
    columns, rows, packs, sems,
):
    copies = fetch(pulse_data, other, here, there, sems, 0)
    for copy in copies:
        copy.start()
    beams = split.shape[1]
    place = scalars[1]
    packs[0, 0:8] = mine[24:32]
    packs[0, 8:16] = jnp.broadcast_to(mine[34:35], (8, beams))
    packs[1, 0:8] = near[8:16]
    packs[1, 8:16] = jnp.broadcast_to(near[18:19], (8, beams))
    packs[2, 0:8] = middle[0:8]
    packs[2, 8:16] = jnp.broadcast_to(middle[10:11], (8, beams))
    packs[3, 0:8] = far[0:8]
    packs[3, 8:16] = jnp.broadcast_to(far[10:11], (8, beams))
    packs[4, 0:8] = mine[16:24]
    packs[4, 8:16] = jnp.broadcast_to(mine[33:34], (8, beams))
    packs[5, 0:8] = near[0:8]
    packs[5, 8:16] = jnp.broadcast_to(near[17:18], (8, beams))
    order = [4 + (x ^ place & 1) for x in range(2)] + [k ^ place for k in range(4)]
    rows[48:56] = jnp.broadcast_to(mine[32:33], (8, beams))
    for unit, source in enumerate(order):
        rows[8 * unit : 8 * unit + 8] = packs[source, 0:8]
        rows[56 + 8 * unit : 64 + 8 * unit] = packs[source, 8:16]
    columns[...] = rows[...].T
    fill_matrices(
        columns, [split.at[u] for u in range(2)] + [join.at[u] for u in range(4)]
    )

    def part(i, _):
        at = pl.ds(pl.multiple_of(i * 16, 16), 16)
        p = columns[at, :]
        lane = lax.broadcasted_iota(jnp.int32, (16, LANES), 1)
        index = (lane + scalars[3]).astype(F32) * (1.0 / ranges)
        for unit in range(7):
            squint = p[:, 48 + 8 * unit : 49 + 8 * unit]
            cosine, sine = cis_turns(squint * index)
            phase[unit, 0, at, :] = cosine
            phase[unit, 1, at, :] = sine
        cosine, sine = cis_turns(p * (LANES / ranges))
        step[0, at, :] = cosine
        step[1, at, :] = sine
        return 0

    lax.fori_loop(0, beams // 16, part, 0)
    for copy in copies:
        copy.wait()


def second_tables(scalars, mine, near, middle, far, pulse_data, other, ranges, chunks):
    beams = mine.shape[1]
    return pl.pallas_call(
        functools.partial(second_kernel, ranges),
        in_specs=[SMEM] + [VMEM] * 4 + [HBM] * 2,
        out_specs=[VMEM] * 6,
        out_shape=[
            jax.ShapeDtypeStruct((2, beams, beams), BF16),
            jax.ShapeDtypeStruct((4, beams, beams), BF16),
            jax.ShapeDtypeStruct((7, 2, beams, LANES), F32),
            jax.ShapeDtypeStruct((2, beams, LANES), F32),
            jax.ShapeDtypeStruct((chunks, beams, 2 * LANES), BF16),
            jax.ShapeDtypeStruct((chunks, beams, 2 * LANES), BF16),
        ],
        scratch_shapes=[
            pltpu.VMEM((beams, LANES), F32),
            pltpu.VMEM((LANES, beams), F32),
            pltpu.VMEM((6, 16, beams), F32),
            pltpu.SemaphoreType.DMA((2, chunks, 2)),
        ],
        compiler_params=pltpu.CompilerParams(vmem_limit_bytes=SMALL_LIMIT * MIB),
        cost_estimate=pl.CostEstimate(
            flops=60 * beams * beams, bytes_accessed=12 * beams * beams, transcendentals=0
        ),
        name="second",
    )(scalars, mine, near, middle, far, pulse_data, other)


def turned(base, value, turn, count):
    c = math.cos(2.0 * math.pi * turn / count)
    s = math.sin(2.0 * math.pi * turn / count)
    real, imag = base
    re, im = value
    for amount, add_re, add_im in ((c, re, im), (s, im, -re)):
        if abs(amount) < 1e-9:
            continue
        if abs(abs(amount) - 1.0) > 1e-9:
            real, imag = real + amount * add_re, imag + amount * add_im
        elif amount > 0.0:
            real, imag = real + add_re, imag + add_im
        else:
            real, imag = real - add_re, imag - add_im
    return real, imag


def main_limit(classes):
    return (8 if classes <= 4 else 40) * MIB


def main_kernel(
    start, classes, more,
    near, far, merge, split, join, azimuth, step, phase_in,
    *refs,
):
    if more:
        pulse_data, other, keep, send, phase, here, there, merged, pair, spread, sems = refs
        copies = fetch(pulse_data, other, here, there, sems, start)
    else:
        keep, send, phase, merged, pair, spread = refs
        copies = []
    for copy in copies:
        copy.start()
    beams = merged.shape[0]
    tile = 512
    tiles = beams // tile
    small = 256

    def rotate(unit, at, total):
        cosine = phase[unit, 0, at, :]
        sine = phase[unit, 1, at, :]
        ahead_c = step[0, at, 48 + 8 * unit : 49 + 8 * unit]
        ahead_s = step[1, at, 48 + 8 * unit : 49 + 8 * unit]
        phase[unit, 0, at, :] = cosine * ahead_c - sine * ahead_s
        phase[unit, 1, at, :] = cosine * ahead_s + sine * ahead_c
        real = total[:, :LANES]
        imag = total[:, LANES:]
        return cosine * real - sine * imag, sine * real + cosine * imag

    def product(lhs, rhs):
        return jnp.dot(lhs, rhs, preferred_element_type=F32)

    def chunk(j, _):
        lanes = pl.ds(pl.multiple_of(j * LANES, LANES), LANES)
        for i in range(tiles):
            at = pl.ds(i * tile, tile)
            real, imag = rotate(
                0, at, product(merge[0, at, :], near[j]) + product(merge[1, at, :], far[j])
            )
            merged[at, :LANES] = real.astype(BF16)
            merged[at, LANES:] = imag.astype(BF16)
        for x in range(2):
            for i in range(tiles):
                at = pl.ds(i * tile, tile)
                real, imag = rotate(1 + x, at, product(split[x, at, :], merged[...]))
                pair[x, at, :LANES] = real.astype(BF16)
                pair[x, at, LANES:] = imag.astype(BF16)
        for i in range(beams // small):
            at = pl.ds(i * small, small)
            terms = [
                rotate(3 + k, at, product(join[k, at, :], pair[k % 2])) for k in range(4)
            ]
            pairs = {}
            for q in range(classes):
                turn = 2 * q % classes
                if turn not in pairs:
                    pairs[turn] = [turned(terms[x], terms[x + 2], turn, classes) for x in range(2)]
                real, imag = turned(*pairs[turn], q, classes)
                spread[q, at, :LANES] = real.astype(BF16)
                spread[q, at, LANES:] = imag.astype(BF16)
        rows = BINS // classes
        half = rows // 2
        for q in range(classes):
            both = product(azimuth[pl.ds(2 * q * rows, 2 * rows), :], spread[q])
            by_cos, by_sin = both[:rows], both[rows:]
            sides = (
                by_cos[:, :LANES] + by_sin[:, LANES:],
                by_cos[:, LANES:] - by_sin[:, :LANES],
            )
            for t, side in enumerate(sides):
                keep[t, q, :, lanes] = side[:half]
                send[t, q, :, lanes] = side[half:].astype(BF16)
        return 0

    lax.fori_loop(0, near.shape[0], chunk, 0)
    for copy in copies:
        copy.wait()


def partial_spectrum(near, far, tables, phase, pulse_data, other, start, chunks, classes):
    beams = near.shape[1]
    width = near.shape[0] * LANES
    half = BINS // classes // 2
    ahead = [jax.ShapeDtypeStruct((chunks, beams, 2 * LANES), BF16)] * 2 if chunks else []
    return pl.pallas_call(
        functools.partial(main_kernel, start, classes, chunks > 0),
        in_specs=[VMEM] * 8 + [HBM] * len(ahead),
        out_specs=[VMEM] * (3 + len(ahead)),
        out_shape=[
            jax.ShapeDtypeStruct((2, classes, half, width), F32),
            jax.ShapeDtypeStruct((2, classes, half, width), BF16),
            jax.ShapeDtypeStruct(phase.shape, F32),
        ]
        + ahead,
        scratch_shapes=[
            pltpu.VMEM((beams, 2 * LANES), BF16),
            pltpu.VMEM((2, beams, 2 * LANES), BF16),
            pltpu.VMEM((classes, beams, 2 * LANES), BF16),
        ]
        + ([pltpu.SemaphoreType.DMA((2, chunks, 2))] if ahead else []),
        input_output_aliases={7: 2},
        compiler_params=pltpu.CompilerParams(vmem_limit_bytes=main_limit(classes)),
        cost_estimate=pl.CostEstimate(
            flops=2 * 20 * beams * beams * width,
            bytes_accessed=beams * beams,
            transcendentals=0,
        ),
        name="main",
    )(near, far, *tables, phase, *([pulse_data, other] if ahead else []))


def covariance_kernel(scale, *refs):
    parts = (len(refs) - 2) // 2
    kept, received = refs[:parts], refs[parts : 2 * parts]
    spectrum, covariance = refs[2 * parts :]
    classes, rows = kept[0].shape[1:3]
    inner = BLOCK // classes
    at = 0
    for h in range(parts):
        width = kept[h].shape[3]
        spectrum[:, :, :, at : at + width] = (
            kept[h][...] + received[h][...].astype(F32)
        ) * scale
        at += width

    def gram(a, b):
        return lax.dot_general(
            a, b, (((1,), (1,)), ((), ())),
            precision=lax.Precision.HIGHEST, preferred_element_type=F32,
        )

    def block(b, _):
        at = pl.ds(pl.multiple_of(b * inner, inner), inner)
        real, imag = [
            jnp.concatenate([spectrum[t, q, at, :] for q in range(classes)], axis=0)
            for t in range(2)
        ]
        covariance[b] = gram(real, jnp.concatenate([real, -imag], axis=0)) + gram(
            imag, jnp.concatenate([imag, real], axis=0)
        )
        return 0

    lax.fori_loop(0, rows // inner, block, 0)


def spectrum_and_covariance(kept, received, scale):
    _, classes, rows, _ = kept[0].shape
    width = sum(part.shape[3] for part in kept)
    inner = BLOCK // classes
    return pl.pallas_call(
        functools.partial(covariance_kernel, scale),
        in_specs=[VMEM] * (2 * len(kept)),
        out_specs=[VMEM, VMEM],
        out_shape=[
            jax.ShapeDtypeStruct((2, classes, rows, width), F32),
            jax.ShapeDtypeStruct((rows // inner, BLOCK, 2 * BLOCK), F32),
        ],
        compiler_params=pltpu.CompilerParams(vmem_limit_bytes=SMALL_LIMIT * MIB),
        name="covariance",
    )(*kept, *received)


def focus_kernel(*refs):
    covs, (spectrum, out, stage) = refs[:-3], refs[-3:]
    classes, rows = spectrum.shape[1:3]
    inner = BLOCK // classes
    factor = math.sqrt(BLOCK)
    lane = lax.broadcasted_iota(jnp.int32, (1, 2 * BLOCK), 1)
    first = lane < BLOCK

    def turned(row):
        return pltpu.roll(jnp.broadcast_to(row, (8, 2 * BLOCK)), BLOCK, 1)[0:1]

    for b in range(rows // inner):
        cov = covs[0][b]
        for other in covs[1:]:
            cov = cov + other[b]
        vec_re = jnp.where(first, 1.0, 0.0)
        vec_im = jnp.zeros((1, 2 * BLOCK), F32)
        for step in range(POWER):
            if step % 2 == 0:
                new_re = jnp.sum(
                    cov * jnp.where(first, vec_re, -turned(vec_im)), axis=1, keepdims=True
                )
                new_im = jnp.sum(
                    cov * jnp.where(first, vec_im, turned(vec_re)), axis=1, keepdims=True
                )
                power = jnp.sum(new_re * new_re + new_im * new_im, axis=0, keepdims=True)
            else:
                by_re = jnp.sum(cov * vec_re, axis=0, keepdims=True)
                by_im = jnp.sum(cov * vec_im, axis=0, keepdims=True)
                new_re = jnp.where(first, by_re + turned(by_im), 0.0)
                new_im = jnp.where(first, by_im - turned(by_re), 0.0)
                power = jnp.sum(new_re * new_re + new_im * new_im, axis=1, keepdims=True)
            length = jnp.sqrt(power + EPSILON)
            vec_re = new_re / length
            vec_im = new_im / length
        for q in range(classes):
            re = spectrum[0, q, b * inner : (b + 1) * inner, :]
            im = spectrum[1, q, b * inner : (b + 1) * inner, :]
            by_re = vec_re[q * inner : (q + 1) * inner] * factor
            by_im = vec_im[q * inner : (q + 1) * inner] * factor
            at = pl.ds(q, inner, stride=classes)
            for t, side in enumerate((re * by_re + im * by_im, im * by_re - re * by_im)):
                for j in range(stage.shape[1]):
                    stage[t, j, at, :] = side[:, j * LANES : (j + 1) * LANES]
        for t in range(2):
            for j in range(stage.shape[1]):
                out[t, b * BLOCK : (b + 1) * BLOCK, j * LANES : (j + 1) * LANES] = stage[t, j]


def focus(covs, spectrum):
    _, classes, rows, ranges = spectrum.shape
    return pl.pallas_call(
        focus_kernel,
        in_specs=[VMEM] * (len(covs) + 1),
        out_specs=VMEM,
        out_shape=jax.ShapeDtypeStruct((2, classes * rows, ranges), F32),
        scratch_shapes=[pltpu.VMEM((2, ranges // LANES, BLOCK, LANES), F32)],
        compiler_params=pltpu.CompilerParams(vmem_limit_bytes=SMALL_LIMIT * MIB),
        name="focus",
    )(*covs, spectrum)


def per_device(pulse_data, merge_taps, merge_weights, squint):
    pulses = lax.axis_size("pulse")
    range_count = lax.axis_size("range")
    pulse_index = lax.axis_index("pulse")
    range_index = lax.axis_index("range")
    _, beams, range_cols = pulse_data.shape
    ranges = range_cols * range_count
    angles = beams * pulses
    classes = pulses // 2
    mine, near, far = pack(merge_taps, merge_weights, squint)
    near = swap(near, "pulse", 2)
    middle = swap(far, "pulse", 4)
    far = swap(far, "pulse", 6)
    other = swap(pulse_data, "pulse", 1)
    scalars = jnp.stack(
        [
            pulse_index,
            pulse_index >> 1 & 3,
            (pulse_index & ~6) * beams,
            range_index * range_cols,
        ]
    )
    merge, azimuth = first_tables(scalars, mine, pulses)
    total = range_cols // LANES
    sizes = [total // 4, total // 4, total // 4, total - total // 8 * 7, total // 8] if total >= 8 else [1] * total
    calls = len(sizes)
    split, join, phase, step, here, there = second_tables(
        scalars, mine, near, middle, far, pulse_data, other, ranges, sizes[0]
    )
    tables = (merge, split, join, azimuth, step)
    stages = pulses.bit_length() - 1
    halves = [None] * calls

    def advance(part):
        keep, arrived, stage = halves[part]
        total = keep + arrived.astype(F32)
        half = total.shape[2] // 2
        send = total[:, :, half:].astype(BF16)
        arrived = swap(send, "pulse", 1 << stage)
        halves[part] = (total[:, :, :half], arrived, stage + 1)
        return send

    for part in range(calls):
        done = [advance(p) for p in range(part - 1) if halves[p][2] < stages]
        if done:
            phase, done = lax.optimization_barrier((phase, done))
        keep, send, phase, *ahead = partial_spectrum(
            here, there, tables, phase, pulse_data, other,
            sum(sizes[: part + 1]) * LANES,
            sizes[part + 1] if part + 1 < calls else 0,
            classes,
        )
        if ahead:
            here, there = ahead
        halves[part] = (keep, swap(send, "pulse", 1), 1)
    for stage in range(1, stages):
        for part in range(calls):
            if halves[part][2] == stage:
                advance(part)
    kept = [half[0] for half in halves]
    received = [half[1] for half in halves]
    spectrum, cov = spectrum_and_covariance(kept, received, angles ** (-0.5))
    covs = [cov]
    distance = 1
    while distance < range_count:
        total = covs[0]
        for extra in covs[1:]:
            total = total + extra
        covs = [total]
        for turn in range(1, min(4, range_count // distance)):
            covs.append(swap(total, "range", turn * distance))
        distance *= 4
    return focus(covs, spectrum)


def solution(mesh):
    placed = (
        P(None, "pulse", "range"),
        P(None, None, None, "pulse"),
        P(None, None, None, "pulse"),
        P(None, "pulse"),
    )
    return jax.shard_map(
        per_device, mesh=mesh, in_specs=placed, out_specs=P(None, "pulse", "range"), check_vma=False
    )
```

profile of v0, /device:TPU:0, one launch (start us, length us, event | category | flops | bytes accessed | tf_op | source)
XLA Modules:
  0.0 143.9 jit_solution(6732931140976872976)
XLA Ops:
  0.5 0.9 copy-done.2
  1.4 0.8 copy-done.3
  2.2 0.7 copy-done.4
  3.0 4.7 %collective-permute-start.2 = (f32[16,1024]{1,0:T(8,128)S(1)}, f32[16,1024]{1,0:T(8,128)S(1)}, u32[]{:S(2)}, u32[]{:S(2)}) collective-permute-start(f32[16,1024]{1,0:T(8,128)S(1)} %get-tuple-element.45), channel_id=1, source_target_pairs={{0,24},{4,28},{8,16},{12,20},{16,8},{20,12},{24,0},{28,4},{1,25},{... | collective-permute-start | bytes 196616 | tf_op jit(solution)/shard_map/ppermute | solution.py:44
  7.6 0.6 collective-permute-start
  8.3 12.0 %first.1 = (bf16[2,1024,1024]{2,1,0:T(8,128)(2,1)S(1)}, bf16[2048,1024]{1,0:T(8,128)(2,1)S(1)}) custom-call(s32[4]{0:T(128)S(1)} %pad_add_fusion.scalars, f32[40,1024]{1,0:T(8,128)S(1)} %get-tuple-element.43.mine), custom_call_target="tpu_custom_call" | custom-call | flops 31457280 | bytes 8388608 | tf_op jit(solution)/shard_map/first/pallas_call | solution.py:155
  20.4 2.2 %copy-done = bf16[2,1024,1024]{2,1,0:T(8,128)(2,1)S(1)} copy-done((bf16[2,1024,1024]{2,1,0:T(8,128)(2,1)S(1)}, bf16[2,1024,1024]{2,1,0:T(8,128)(2,1)}, u32[]{:S(2)}) %copy-start) | copy-done | bytes 4194328
  22.6 19.5 %second.1 = (bf16[2,1024,1024]{2,1,0:T(8,128)(2,1)S(1)}, bf16[4,1024,1024]{2,1,0:T(8,128)(2,1)S(1)}, f32[7,2,1024,128]{3,2,1,0:T(8,128)S(1)}, f32[2,1024,128]{2,...) custom-call(s32[4]{0:T(128)S(1)} %pad_add_fusion.scalars, ...), custom_call_target="tpu_custom_call" | custom-call | flops 62914560 | bytes 12582912 | tf_op jit(solution)/shard_map/second/pallas_call | solution.py:240
  42.0 13.5 %main.5 = (f32[2,4,128,256]{3,2,1,0:T(8,128)S(1)}, bf16[2,4,128,256]{3,2,1,0:T(8,128)(2,1)S(1)}, f32[7,2,1024,128]{3,2,1,0:T(8,128)S(1)}, bf16[2,1024,256]{2,1,0:T(8,128)(2,1)S(1)}, bf16[2,1024,256]{2,1,0:T(8,128)(2,1)S(1)}) custom-call(bf16[2,1024,256]{2,1,0:T(8,128)(2,1)S(1)} %get-tuple-element.46.near, ...), custom_call_target="tpu_custom_call", output_to_operand_aliasing={{2}: (7, {})} | custom-call | flops 10737418240 | bytes 1048576 | tf_op jit(solution)/shard_map/main/pallas_call | solution.py:371
  55.7 13.7 %main.6 = (f32[2,4,128,256]{3,2,1,0:T(8,128)S(1)}, bf16[2,4,128,256]{3,2,1,0:T(8,128)(2,1)S(1)}, f32[7,2,1024,128]{3,2,1,0:T(8,128)S(1)}, bf16[2,1024,256]{2,1,0:T(8,128)(2,1)S(1)}, bf16[2,1024,256]{2,1,0:T(8,128)(2,1)S(1)}) custom-call(bf16[2,1024,256]{2,1,0:T(8,128)(2,1)S(1)} %get-tuple-element.56.near, ...), custom_call_target="tpu_custom_call", output_to_operand_aliasing={{2}: (7, {})} | custom-call | flops 10737418240 | bytes 1048576 | tf_op jit(solution)/shard_map/main/pallas_call | solution.py:371
  69.4 0.6 collective-permute-start.6
  70.1 1.5 %collective-permute-start.5 = (bf16[2,4,64,256]{3,2,1,0:T(8,128)(2,1)S(1)}, bf16[2,4,64,256]{3,2,1,0:T(8,128)(2,1)S(1)}, u32[]{:S(2)}, u32[]{:S(2)}) collective-permute-start(bf16[2,4,64,256]{3,2,1,0:T(8,128)(2,1)S(1)} %slice.127), channel_id=1, source_target_pairs={{0,8},{4,12},{8,0},{12,4},{16,24},{20,28},{24,16},{28,20},{1,9},{5... | collective-permute-start | bytes 786440 | tf_op jit(solution)/shard_map/ppermute | solution.py:44
  71.5 13.5 %main.7 = (f32[2,4,128,256]{3,2,1,0:T(8,128)S(1)}, bf16[2,4,128,256]{3,2,1,0:T(8,128)(2,1)S(1)}, f32[7,2,1024,128]{3,2,1,0:T(8,128)S(1)}, bf16[1,1024,256]{2,1,0:T(8,128)(2,1)S(1)}, bf16[1,1024,256]{2,1,0:T(8,128)(2,1)S(1)}) custom-call(bf16[2,1024,256]{2,1,0:T(8,128)(2,1)S(1)} %get-tuple-element.61.near, ...), custom_call_target="tpu_custom_call", output_to_operand_aliasing={{2}: (7, {})} | custom-call | flops 10737418240 | bytes 1048576 | tf_op jit(solution)/shard_map/main/pallas_call | solution.py:371
  85.3 0.7 collective-permute-start.7
  86.1 7.6 %main.8 = (f32[2,4,128,128]{3,2,1,0:T(8,128)S(1)}, bf16[2,4,128,128]{3,2,1,0:T(8,128)(2,1)S(1)}, f32[7,2,1024,128]{3,2,1,0:T(8,128)S(1)}, bf16[1,1024,256]{2,1,0:T(8,128)(2,1)S(1)}, bf16[1,1024,256]{2,1,0:T(8,128)(2,1)S(1)}) custom-call(bf16[1,1024,256]{2,1,0:T(8,128)(2,1)S(1)} %get-tuple-element.67.near, ...), custom_call_target="tpu_custom_call", output_to_operand_aliasing={{2}: (7, {})} | custom-call | flops 5368709120 | bytes 1048576 | tf_op jit(solution)/shard_map/main/pallas_call | solution.py:371
  94.4 1.0 collective-permute-done.10
  95.5 1.4 %collective-permute-start.11 = (bf16[2,4,64,128]{3,2,1,0:T(8,128)(2,1)S(1)}, bf16[2,4,64,128]{3,2,1,0:T(8,128)(2,1)S(1)}, u32[]{:S(2)}, u32[]{:S(2)}) collective-permute-start(bf16[2,4,64,128]{3,2,1,0:T(8,128)(2,1)S(1)} %slice.131), channel_id=1, source_target_pairs={{0,8},{4,12},{8,0},{12,4},{16,24},{20,28},{24,16},{28,20},{1,9},{5... | collective-permute-start | bytes 393224 | tf_op jit(solution)/shard_map/ppermute | solution.py:44
  96.9 6.9 %main.9 = (f32[2,4,128,128]{3,2,1,0:T(8,128)S(1)}, bf16[2,4,128,128]{3,2,1,0:T(8,128)(2,1)S(1)}, f32[7,2,1024,128]{3,2,1,0:T(8,128)S(1)}) custom-call(bf16[1,1024,256]{2,1,0:T(8,128)(2,1)S(1)} %get-tuple-element.73.near, bf16[1,1024,256]{2,1,0:T(8,128)(2,1)S(1)} %get-tuple-element.74.far, ...), custom_call_target="tpu_custom_call", output_to_operand_aliasing={{2}: (7, {})} | custom-call | flops 5368709120 | bytes 1048576 | tf_op jit(solution)/shard_map/main/pallas_call | solution.py:371
  103.9 3.0 %collective-permute-start.14 = (bf16[2,4,32,256]{3,2,1,0:T(8,128)(2,1)S(1)}, bf16[2,4,32,256]{3,2,1,0:T(8,128)(2,1)S(1)}, u32[]{:S(2)}, u32[]{:S(2)}) collective-permute-start(bf16[2,4,32,256]{3,2,1,0:T(8,128)(2,1)S(1)} %slice.132), channel_id=1, source_target_pairs={{0,16},{4,20},{8,24},{12,28},{16,0},{20,4},{24,8},{28,12},{1,17},{... | collective-permute-start | bytes 393224 | tf_op jit(solution)/shard_map/ppermute | solution.py:44
  106.9 0.6 collective-permute-start.9
  107.5 2.5 %collective-permute-start.17 = (bf16[2,4,32,128]{3,2,1,0:T(8,128)(2,1)S(1)}, bf16[2,4,32,128]{3,2,1,0:T(8,128)(2,1)S(1)}, u32[]{:S(2)}, u32[]{:S(2)}) collective-permute-start(bf16[2,4,32,128]{3,2,1,0:T(8,128)(2,1)S(1)} %slice.134), channel_id=1, source_target_pairs={{0,16},{4,20},{8,24},{12,28},{16,0},{20,4},{24,8},{28,12},{1,17},{... | collective-permute-start | bytes 196616 | tf_op jit(solution)/shard_map/ppermute | solution.py:44
  110.1 1.9 %collective-permute-start.13 = (bf16[2,4,64,128]{3,2,1,0:T(8,128)(2,1)S(1)}, bf16[2,4,64,128]{3,2,1,0:T(8,128)(2,1)S(1)}, u32[]{:S(2)}, u32[]{:S(2)}) collective-permute-start(bf16[2,4,64,128]{3,2,1,0:T(8,128)(2,1)S(1)} %slice.129), channel_id=1, source_target_pairs={{0,8},{4,12},{8,0},{12,4},{16,24},{20,28},{24,16},{28,20},{1,9},{5... | collective-permute-start | bytes 393224 | tf_op jit(solution)/shard_map/ppermute | solution.py:44
  112.1 10.9 %collective-permute-done.9 = bf16[2,4,64,256]{3,2,1,0:T(8,128)(2,1)S(1)} collective-permute-done((bf16[2,4,64,256]{3,2,1,0:T(8,128)(2,1)S(1)}, bf16[2,4,64,256]{3,2,1,0:T(8,128)(2,1)S(1)}, u32[]{:S(2)}, u32[]{:S(2)}) %collective-permute-start.9) | collective-permute-done | bytes 262176 | tf_op jit(solution)/shard_map/ppermute | solution.py:44
  123.2 1.9 %collective-permute-done.13 = bf16[2,4,64,128]{3,2,1,0:T(8,128)(2,1)S(1)} collective-permute-done((bf16[2,4,64,128]{3,2,1,0:T(8,128)(2,1)S(1)}, bf16[2,4,64,128]{3,2,1,0:T(8,128)(2,1)S(1)}, u32[]{:S(2)}, u32[]{:S(2)}) %collective-permute-start.13) | collective-permute-done | bytes 131104 | tf_op jit(solution)/shard_map/ppermute | solution.py:44
  125.2 1.0 collective-permute-start.18
  126.4 5.2 %collective-permute-done.16.refs_7_ = bf16[2,4,32,256]{3,2,1,0:T(8,128)(2,1)S(1)} collective-permute-done((bf16[2,4,32,256]{3,2,1,0:T(8,128)(2,1)S(1)}, bf16[2,4,32,256]{3,2,1,0:T(8,128)(2,1)S(1)}, u32[]{:S(2)}, u32[]{:S(2)}) %collective-permute-start.16) | collective-permute-done | bytes 131104 | tf_op jit(solution)/shard_map/ppermute | solution.py:44
  131.5 0.7 collective-permute-done.18.refs_9_
  132.2 2.5 %covariance.1 = (f32[2,4,32,1024]{3,2,1,0:T(8,128)S(1)}, f32[2,64,128]{2,1,0:T(8,128)S(1)}) custom-call(f32[2,4,32,256]{3,2,1,0:T(8,128)S(1)} %slice.92.refs_0_, f32[2,4,32,256]{3,2,1,0:T(8,128)S(1)} %slice.95.refs_1_, f32[2,4,32,256]{3,2,1,0:T(8,128)S(1)} %slice.98.refs_2_, f32[2,4,32,128]{3,2,1,0:T(8,128)S(1)} %slice.102.refs_3_, ...), custom_call_target="tpu_custom_call" | custom-call | tf_op jit(solution)/shard_map/covariance/pallas_call | solution.py:436
  134.8 2.5 %collective-permute-start.21 = (f32[2,64,128]{2,1,0:T(8,128)S(1)}, f32[2,64,128]{2,1,0:T(8,128)S(1)}, u32[]{:S(2)}, u32[]{:S(2)}) collective-permute-start(f32[2,64,128]{2,1,0:T(8,128)S(1)} %get-tuple-element.79.refs_0_), channel_id=1, source_target_pairs={{0,3},{1,2},{2,1},{3,0},{4,7},{5,6},{6,5},{7,4},{8,11},{9,10},{10,... | collective-permute-start | bytes 196616 | tf_op jit(solution)/shard_map/ppermute | solution.py:44
  138.3 2.1 %collective-permute-done.21.refs_3_ = f32[2,64,128]{2,1,0:T(8,128)S(1)} collective-permute-done((f32[2,64,128]{2,1,0:T(8,128)S(1)}, f32[2,64,128]{2,1,0:T(8,128)S(1)}, u32[]{:S(2)}, u32[]{:S(2)}) %collective-permute-start.21) | collective-permute-done | bytes 65568 | tf_op jit(solution)/shard_map/ppermute | solution.py:44
  140.4 1.1 collective-permute-done.20.refs_2_
  142.0 1.8 %focus.1 = f32[2,128,1024]{2,1,0:T(8,128)} custom-call(f32[2,64,128]{2,1,0:T(8,128)S(1)} %get-tuple-element.79.refs_0_, f32[2,64,128]{2,1,0:T(8,128)S(1)} %collective-permute-done.19.refs_1_, f32[2,64,128]{2,1,0:T(8,128)S(1)} %collective-permute-done.20.refs_2_, f32[2,64,128]{2,1,0:T(8,128)S(1)} %collective-permute-done.21.refs_3_, ...), custom_call_target="tpu_custom_call" | custom-call | tf_op jit(solution)/shard_map/focus/pallas_call | solution.py:500
  (58 shorter events, 3.8 us)
Async XLA Ops:
  0.0 20.4 %collective-permute-start.3 = (bf16[2,1024,1024]{2,1,0:T(8,128)(2,1)}, bf16[2,1024,1024]{2,1,0:T(8,128)(2,1)}, u32[]{:S(2)}, u32[]{:S(2)}) collective-permute-start(bf16[2,1024,1024]{2,1,0:T(8,128)(2,1)} %refs_0_.7), channel_id=1, source_target_pairs={{0,4},{4,0},{8,12},{12,8},{16,20},{20,16},{24,28},{28,24},{1,5},{5... | collective-permute-start | bytes 12582920 | tf_op jit(solution)/shard_map/ppermute | solution.py:44
  0.5 0.9 copy-start.2
  1.4 0.8 copy-start.3
  2.2 0.7 copy-start.4
  3.0 17.4 %collective-permute-start.2 = (f32[16,1024]{1,0:T(8,128)S(1)}, f32[16,1024]{1,0:T(8,128)S(1)}, u32[]{:S(2)}, u32[]{:S(2)}) collective-permute-start(f32[16,1024]{1,0:T(8,128)S(1)} %get-tuple-element.45), channel_id=1, source_target_pairs={{0,24},{4,28},{8,16},{12,20},{16,8},{20,12},{24,0},{28,4},{1,25},{... | collective-permute-start | bytes 196616 | tf_op jit(solution)/shard_map/ppermute | solution.py:44
  7.6 12.7 %collective-permute-start.1 = (f32[16,1024]{1,0:T(8,128)S(1)}, f32[16,1024]{1,0:T(8,128)S(1)}, u32[]{:S(2)}, u32[]{:S(2)}) collective-permute-start(f32[16,1024]{1,0:T(8,128)S(1)} %get-tuple-element.45), channel_id=1, source_target_pairs={{0,16},{4,20},{8,24},{12,28},{16,0},{20,4},{24,8},{28,12},{1,17},{... | collective-permute-start | bytes 196616 | tf_op jit(solution)/shard_map/ppermute | solution.py:44
  7.6 12.8 %collective-permute-start = (f32[24,1024]{1,0:T(8,128)S(1)}, f32[24,1024]{1,0:T(8,128)S(1)}, u32[]{:S(2)}, u32[]{:S(2)}) collective-permute-start(f32[24,1024]{1,0:T(8,128)S(1)} %get-tuple-element.44), channel_id=1, source_target_pairs={{0,8},{4,12},{8,0},{12,4},{16,24},{20,28},{24,16},{28,20},{1,9},{5... | collective-permute-start | bytes 294920 | tf_op jit(solution)/shard_map/ppermute | solution.py:44
  20.4 2.2 %copy-start = (bf16[2,1024,1024]{2,1,0:T(8,128)(2,1)S(1)}, bf16[2,1024,1024]{2,1,0:T(8,128)(2,1)}, u32[]{:S(2)}) copy-start(bf16[2,1024,1024]{2,1,0:T(8,128)(2,1)} %refs_0_.7) | copy-start | bytes 12582916
  22.6 19.5 %copy-start.1 = (bf16[2,1024,1024]{2,1,0:T(8,128)(2,1)S(1)}, bf16[2,1024,1024]{2,1,0:T(8,128)(2,1)}, u32[]{:S(2)}) copy-start(bf16[2,1024,1024]{2,1,0:T(8,128)(2,1)} %refs_0_.7) | copy-start | bytes 12582916
  55.6 14.3 %collective-permute-start.4 = (bf16[2,4,128,256]{3,2,1,0:T(8,128)(2,1)S(1)}, bf16[2,4,128,256]{3,2,1,0:T(8,128)(2,1)S(1)}, u32[]{:S(2)}, u32[]{:S(2)}) collective-permute-start(bf16[2,4,128,256]{3,2,1,0:T(8,128)(2,1)S(1)} %get-tuple-element.55), channel_id=1, source_target_pairs={{0,4},{4,0},{8,12},{12,8},{16,20},{20,16},{24,28},{28,24},{1,5},{5... | collective-permute-start | bytes 1572872 | tf_op jit(solution)/shard_map/ppermute | solution.py:44
  69.4 15.8 %collective-permute-start.6 = (bf16[2,4,128,256]{3,2,1,0:T(8,128)(2,1)S(1)}, bf16[2,4,128,256]{3,2,1,0:T(8,128)(2,1)S(1)}, u32[]{:S(2)}, u32[]{:S(2)}) collective-permute-start(bf16[2,4,128,256]{3,2,1,0:T(8,128)(2,1)S(1)} %get-tuple-element.60), channel_id=1, source_target_pairs={{0,4},{4,0},{8,12},{12,8},{16,20},{20,16},{24,28},{28,24},{1,5},{5... | collective-permute-start | bytes 1572872 | tf_op jit(solution)/shard_map/ppermute | solution.py:44
  70.1 16.0 %collective-permute-start.5 = (bf16[2,4,64,256]{3,2,1,0:T(8,128)(2,1)S(1)}, bf16[2,4,64,256]{3,2,1,0:T(8,128)(2,1)S(1)}, u32[]{:S(2)}, u32[]{:S(2)}) collective-permute-start(bf16[2,4,64,256]{3,2,1,0:T(8,128)(2,1)S(1)} %slice.127), channel_id=1, source_target_pairs={{0,8},{4,12},{8,0},{12,4},{16,24},{20,28},{24,16},{28,20},{1,9},{5... | collective-permute-start | bytes 786440 | tf_op jit(solution)/shard_map/ppermute | solution.py:44
  85.1 9.1 %collective-permute-start.8 = (bf16[2,4,128,256]{3,2,1,0:T(8,128)(2,1)S(1)}, bf16[2,4,128,256]{3,2,1,0:T(8,128)(2,1)S(1)}, u32[]{:S(2)}, u32[]{:S(2)}) collective-permute-start(bf16[2,4,128,256]{3,2,1,0:T(8,128)(2,1)S(1)} %get-tuple-element.66), channel_id=1, source_target_pairs={{0,4},{4,0},{8,12},{12,8},{16,20},{20,16},{24,28},{28,24},{1,5},{5... | collective-permute-start | bytes 1572872 | tf_op jit(solution)/shard_map/ppermute | solution.py:44
  85.3 8.8 %collective-permute-start.7 = (bf16[2,4,64,256]{3,2,1,0:T(8,128)(2,1)S(1)}, bf16[2,4,64,256]{3,2,1,0:T(8,128)(2,1)S(1)}, u32[]{:S(2)}, u32[]{:S(2)}) collective-permute-start(bf16[2,4,64,256]{3,2,1,0:T(8,128)(2,1)S(1)} %slice.126), channel_id=1, source_target_pairs={{0,8},{4,12},{8,0},{12,4},{16,24},{20,28},{24,16},{28,20},{1,9},{5... | collective-permute-start | bytes 786440 | tf_op jit(solution)/shard_map/ppermute | solution.py:44
  93.8 1.6 %collective-permute-start.10 = (bf16[2,4,128,128]{3,2,1,0:T(8,128)(2,1)S(1)}, bf16[2,4,128,128]{3,2,1,0:T(8,128)(2,1)S(1)}, u32[]{:S(2)}, u32[]{:S(2)}) collective-permute-start(bf16[2,4,128,128]{3,2,1,0:T(8,128)(2,1)S(1)} %get-tuple-element.72), channel_id=1, source_target_pairs={{0,4},{4,0},{8,12},{12,8},{16,20},{20,16},{24,28},{28,24},{1,5},{5... | collective-permute-start | bytes 786440 | tf_op jit(solution)/shard_map/ppermute | solution.py:44
  95.5 12.0 %collective-permute-start.11 = (bf16[2,4,64,128]{3,2,1,0:T(8,128)(2,1)S(1)}, bf16[2,4,64,128]{3,2,1,0:T(8,128)(2,1)S(1)}, u32[]{:S(2)}, u32[]{:S(2)}) collective-permute-start(bf16[2,4,64,128]{3,2,1,0:T(8,128)(2,1)S(1)} %slice.131), channel_id=1, source_target_pairs={{0,8},{4,12},{8,0},{12,4},{16,24},{20,28},{24,16},{28,20},{1,9},{5... | collective-permute-start | bytes 393224 | tf_op jit(solution)/shard_map/ppermute | solution.py:44
  103.8 6.3 %collective-permute-start.12 = (bf16[2,4,128,128]{3,2,1,0:T(8,128)(2,1)S(1)}, bf16[2,4,128,128]{3,2,1,0:T(8,128)(2,1)S(1)}, u32[]{:S(2)}, u32[]{:S(2)}) collective-permute-start(bf16[2,4,128,128]{3,2,1,0:T(8,128)(2,1)S(1)} %get-tuple-element.78), channel_id=1, source_target_pairs={{0,4},{4,0},{8,12},{12,8},{16,20},{20,16},{24,28},{28,24},{1,5},{5... | collective-permute-start | bytes 786440 | tf_op jit(solution)/shard_map/ppermute | solution.py:44
  103.9 22.5 %collective-permute-start.14 = (bf16[2,4,32,256]{3,2,1,0:T(8,128)(2,1)S(1)}, bf16[2,4,32,256]{3,2,1,0:T(8,128)(2,1)S(1)}, u32[]{:S(2)}, u32[]{:S(2)}) collective-permute-start(bf16[2,4,32,256]{3,2,1,0:T(8,128)(2,1)S(1)} %slice.132), channel_id=1, source_target_pairs={{0,16},{4,20},{8,24},{12,28},{16,0},{20,4},{24,8},{28,12},{1,17},{... | collective-permute-start | bytes 393224 | tf_op jit(solution)/shard_map/ppermute | solution.py:44
  106.8 19.5 %collective-permute-start.15 = (bf16[2,4,32,256]{3,2,1,0:T(8,128)(2,1)S(1)}, bf16[2,4,32,256]{3,2,1,0:T(8,128)(2,1)S(1)}, u32[]{:S(2)}, u32[]{:S(2)}) collective-permute-start(bf16[2,4,32,256]{3,2,1,0:T(8,128)(2,1)S(1)} %slice.130), channel_id=1, source_target_pairs={{0,16},{4,20},{8,24},{12,28},{16,0},{20,4},{24,8},{28,12},{1,17},{... | collective-permute-start | bytes 393224 | tf_op jit(solution)/shard_map/ppermute | solution.py:44
  106.9 16.1 %collective-permute-start.9 = (bf16[2,4,64,256]{3,2,1,0:T(8,128)(2,1)S(1)}, bf16[2,4,64,256]{3,2,1,0:T(8,128)(2,1)S(1)}, u32[]{:S(2)}, u32[]{:S(2)}) collective-permute-start(bf16[2,4,64,256]{3,2,1,0:T(8,128)(2,1)S(1)} %slice.125), channel_id=1, source_target_pairs={{0,8},{4,12},{8,0},{12,4},{16,24},{20,28},{24,16},{28,20},{1,9},{5... | collective-permute-start | bytes 786440 | tf_op jit(solution)/shard_map/ppermute | solution.py:44
  107.5 18.8 %collective-permute-start.17 = (bf16[2,4,32,128]{3,2,1,0:T(8,128)(2,1)S(1)}, bf16[2,4,32,128]{3,2,1,0:T(8,128)(2,1)S(1)}, u32[]{:S(2)}, u32[]{:S(2)}) collective-permute-start(bf16[2,4,32,128]{3,2,1,0:T(8,128)(2,1)S(1)} %slice.134), channel_id=1, source_target_pairs={{0,16},{4,20},{8,24},{12,28},{16,0},{20,4},{24,8},{28,12},{1,17},{... | collective-permute-start | bytes 196616 | tf_op jit(solution)/shard_map/ppermute | solution.py:44
  110.1 15.0 %collective-permute-start.13 = (bf16[2,4,64,128]{3,2,1,0:T(8,128)(2,1)S(1)}, bf16[2,4,64,128]{3,2,1,0:T(8,128)(2,1)S(1)}, u32[]{:S(2)}, u32[]{:S(2)}) collective-permute-start(bf16[2,4,64,128]{3,2,1,0:T(8,128)(2,1)S(1)} %slice.129), channel_id=1, source_target_pairs={{0,8},{4,12},{8,0},{12,4},{16,24},{20,28},{24,16},{28,20},{1,9},{5... | collective-permute-start | bytes 393224 | tf_op jit(solution)/shard_map/ppermute | solution.py:44
  123.1 8.4 %collective-permute-start.16 = (bf16[2,4,32,256]{3,2,1,0:T(8,128)(2,1)S(1)}, bf16[2,4,32,256]{3,2,1,0:T(8,128)(2,1)S(1)}, u32[]{:S(2)}, u32[]{:S(2)}) collective-permute-start(bf16[2,4,32,256]{3,2,1,0:T(8,128)(2,1)S(1)} %slice.128), channel_id=1, source_target_pairs={{0,16},{4,20},{8,24},{12,28},{16,0},{20,4},{24,8},{28,12},{1,17},{... | collective-permute-start | bytes 393224 | tf_op jit(solution)/shard_map/ppermute | solution.py:44
  125.2 7.1 %collective-permute-start.18 = (bf16[2,4,32,128]{3,2,1,0:T(8,128)(2,1)S(1)}, bf16[2,4,32,128]{3,2,1,0:T(8,128)(2,1)S(1)}, u32[]{:S(2)}, u32[]{:S(2)}) collective-permute-start(bf16[2,4,32,128]{3,2,1,0:T(8,128)(2,1)S(1)} %slice.133), channel_id=1, source_target_pairs={{0,16},{4,20},{8,24},{12,28},{16,0},{20,4},{24,8},{28,12},{1,17},{... | collective-permute-start | bytes 196616 | tf_op jit(solution)/shard_map/ppermute | solution.py:44
  134.8 5.7 %collective-permute-start.21 = (f32[2,64,128]{2,1,0:T(8,128)S(1)}, f32[2,64,128]{2,1,0:T(8,128)S(1)}, u32[]{:S(2)}, u32[]{:S(2)}) collective-permute-start(f32[2,64,128]{2,1,0:T(8,128)S(1)} %get-tuple-element.79.refs_0_), channel_id=1, source_target_pairs={{0,3},{1,2},{2,1},{3,0},{4,7},{5,6},{6,5},{7,4},{8,11},{9,10},{10,... | collective-permute-start | bytes 196616 | tf_op jit(solution)/shard_map/ppermute | solution.py:44
  137.3 4.3 %collective-permute-start.20 = (f32[2,64,128]{2,1,0:T(8,128)S(1)}, f32[2,64,128]{2,1,0:T(8,128)S(1)}, u32[]{:S(2)}, u32[]{:S(2)}) collective-permute-start(f32[2,64,128]{2,1,0:T(8,128)S(1)} %get-tuple-element.79.refs_0_), channel_id=1, source_target_pairs={{0,2},{1,3},{2,0},{3,1},{4,6},{5,7},{6,4},{7,5},{8,10},{9,11},{10,... | collective-permute-start | bytes 196616 | tf_op jit(solution)/shard_map/ppermute | solution.py:44
  137.8 4.3 %collective-permute-start.19 = (f32[2,64,128]{2,1,0:T(8,128)S(1)}, f32[2,64,128]{2,1,0:T(8,128)S(1)}, u32[]{:S(2)}, u32[]{:S(2)}) collective-permute-start(f32[2,64,128]{2,1,0:T(8,128)S(1)} %get-tuple-element.79.refs_0_), channel_id=1, source_target_pairs={{0,1},{1,0},{2,3},{3,2},{4,5},{5,4},{6,7},{7,6},{8,9},{9,8},{10,11... | collective-permute-start | bytes 196616 | tf_op jit(solution)/shard_map/ppermute | solution.py:44
where the time goes:
time: 144 us
  Pallas kernels  91.1 us (63%)
  waiting for transfers between devices  23.6 us (16%)
  starting transfers between devices  23.2 us (16%)
  local copies, waits for them, and re-layouts  4.87 us (3%)
    pallas_call x5, Pallas kernels, partial_spectrum(): pl.pallas_call(functools.partial(main_kernel, start, classes, chunks > 0)...  55.3 us
    ppermute x22, waiting for transfers between devices, swap(): return lax.ppermute(block, axis, [(i, i ^ distance) for i in range(count)])  23.6 us
    ppermute x22, starting transfers between devices, swap(): return lax.ppermute(block, axis, [(i, i ^ distance) for i in range(count)])  23.2 us
    pallas_call x1, Pallas kernels, second_tables(): pl.pallas_call(functools.partial(second_kernel, ranges), in_specs=[SMEM]...  19.5 us
    pallas_call x1, Pallas kernels, first_tables(): pl.pallas_call(functools.partial(first_kernel, pulses), in_specs=[SMEM, V...  12 us
    unnamed x10, local copies, waits for them, and re-layouts  4.59 us
  transfers between devices with their start and end apart: 22, of which 8 were waited for; matrix products, arithmetic and copies ran while one was open for 1% of the time, Pallas kernels for 37%

commit v1 on v0

--- a/solution.py
+++ b/solution.py
@@ -88,14 +88,15 @@
         at = pl.ds(pl.multiple_of(i * 16, 16), 16)
         lane = lax.broadcasted_iota(jnp.int32, (16, LANES), 1)
         lanes = [(lane + j * LANES).astype(jnp.int16) for j in range(beams // LANES)]
-        p = columns[at, :]
-
-        def spread(column):
-            return jnp.broadcast_to(p[:, column : column + 1], (16, LANES))
+        whole = columns[at, :].astype(jnp.int32).astype(jnp.int16)
+        real = columns[at, :].astype(BF16)
+
+        def spread(value, column):
+            return jnp.broadcast_to(value[:, column : column + 1], (16, LANES))
 
         for unit, out in enumerate(outs):
-            taps = [spread(8 * unit + c).astype(jnp.int32).astype(jnp.int16) for c in range(4)]
-            weights = [spread(8 * unit + 4 + c).astype(BF16) for c in range(4)]
+            taps = [spread(whole, 8 * unit + c) for c in range(4)]
+            weights = [spread(real, 8 * unit + 4 + c) for c in range(4)]
             for j, here in enumerate(lanes):
                 total = jnp.zeros((16, LANES), BF16)
                 for tap, weight in zip(taps, weights):
@@ -132,19 +133,21 @@
         )
         lane = lax.broadcasted_iota(jnp.int32, (16, LANES), 1)
         whole = angles - 1
-        fine_c, fine_s = cis_turns((bins * lane & whole).astype(F32) * (1.0 / angles))
-        coarse_c, coarse_s = cis_turns(
-            (bins * (scalars[2] + lane * LANES & whole) & whole).astype(F32) * (1.0 / angles)
+        cosine, sine = cis_turns(
+            (bins * (scalars[2] + lane & whole) & whole).astype(F32) * (1.0 / angles)
         )
+        ahead_c, ahead_s = cis_turns((bins * LANES & whole).astype(F32) * (1.0 / angles))
         low = i * 16 + (i * 16 >> (count.bit_length() - 1)) * count
         cos_at = pl.ds(pl.multiple_of(low, 16), 16)
         sin_at = pl.ds(pl.multiple_of(low + count, 16), 16)
         for j in range(beams // LANES):
-            a_c = coarse_c[:, j : j + 1]
-            a_s = coarse_s[:, j : j + 1]
             lanes = slice(j * LANES, (j + 1) * LANES)
-            table[cos_at, lanes] = (a_c * fine_c - a_s * fine_s).astype(BF16)
-            table[sin_at, lanes] = (a_s * fine_c + a_c * fine_s).astype(BF16)
+            table[cos_at, lanes] = cosine.astype(BF16)
+            table[sin_at, lanes] = sine.astype(BF16)
+            cosine, sine = (
+                cosine * ahead_c - sine * ahead_s,
+                sine * ahead_c + cosine * ahead_s,
+            )
         return 0
 
     lax.fori_loop(0, BINS // 16, part, 0, unroll=2)

time: 144 us -> 138 us (0.958)
  Pallas kernels: 91.1 us -> 84.7 us
    pallas_call x1, Pallas kernels: 12 us -> 7.95 us  [first_tables(): pl.pallas_call(functools.partial(first_kernel, pulses), in_specs=[SMEM, V...]
    pallas_call x1, Pallas kernels: 19.5 us -> 17.1 us  [second_tables(): pl.pallas_call(functools.partial(second_kernel, ranges), in_specs=[SMEM]...]
  transfers between devices with their start and end apart: 22 -> 22, of which waited for: 8 -> 9; matrix products, arithmetic and copies ran while one was open for 1% -> 1% of each run, Pallas kernels for 37% -> 36%
where the time goes in v1:
time: 138 us; the launch traced here: 137 us
  Pallas kernels  84.7 us (61%)
  waiting for transfers between devices  23.6 us (17%)
  starting transfers between devices  23.2 us (17%)
  local copies, waits for them, and re-layouts  4.87 us (4%)
    pallas_call x5, Pallas kernels, partial_spectrum(): pl.pallas_call(functools.partial(main_kernel, start, classes, chunks > 0)...  55.2 us
    ppermute x22, waiting for transfers between devices, swap(): return lax.ppermute(block, axis, [(i, i ^ distance) for i in range(count)])  23.6 us
    ppermute x22, starting transfers between devices, swap(): return lax.ppermute(block, axis, [(i, i ^ distance) for i in range(count)])  23.2 us
    pallas_call x1, Pallas kernels, second_tables(): pl.pallas_call(functools.partial(second_kernel, ranges), in_specs=[SMEM]...  17.1 us
    pallas_call x1, Pallas kernels, first_tables(): pl.pallas_call(functools.partial(first_kernel, pulses), in_specs=[SMEM, V...  7.95 us
    unnamed x10, local copies, waits for them, and re-layouts  4.59 us
  transfers between devices with their start and end apart: 22, of which 9 were waited for; matrix products, arithmetic and copies ran while one was open for 1% of the time, Pallas kernels for 36%

profile of v1, /device:TPU:0, one launch (start us, length us, event | category | flops | bytes accessed | tf_op | source)
XLA Modules:
  0.0 137.5 jit_solution(6038457470998531933)
XLA Ops:
  0.5 0.9 copy-done.2
  1.4 0.8 copy-done.3
  2.2 0.7 copy-done.4
  3.0 4.7 %collective-permute-start.2 = (f32[16,1024]{1,0:T(8,128)S(1)}, f32[16,1024]{1,0:T(8,128)S(1)}, u32[]{:S(2)}, u32[]{:S(2)}) collective-permute-start(f32[16,1024]{1,0:T(8,128)S(1)} %get-tuple-element.45), channel_id=1, source_target_pairs={{0,24},{4,28},{8,16},{12,20},{16,8},{20,12},{24,0},{28,4},{1,25},{... | collective-permute-start | bytes 196616 | tf_op jit(solution)/shard_map/ppermute | solution.py:44
  7.6 0.6 collective-permute-start
  8.3 7.9 %first.1 = (bf16[2,1024,1024]{2,1,0:T(8,128)(2,1)S(1)}, bf16[2048,1024]{1,0:T(8,128)(2,1)S(1)}) custom-call(s32[4]{0:T(128)S(1)} %pad_add_fusion.scalars, f32[40,1024]{1,0:T(8,128)S(1)} %get-tuple-element.43.mine), custom_call_target="tpu_custom_call" | custom-call | flops 31457280 | bytes 8388608 | tf_op jit(solution)/shard_map/first/pallas_call | solution.py:158
  16.3 2.2 %copy-done = bf16[2,1024,1024]{2,1,0:T(8,128)(2,1)S(1)} copy-done((bf16[2,1024,1024]{2,1,0:T(8,128)(2,1)S(1)}, bf16[2,1024,1024]{2,1,0:T(8,128)(2,1)}, u32[]{:S(2)}) %copy-start) | copy-done | bytes 4194328
  18.5 17.1 %second.1 = (bf16[2,1024,1024]{2,1,0:T(8,128)(2,1)S(1)}, bf16[4,1024,1024]{2,1,0:T(8,128)(2,1)S(1)}, f32[7,2,1024,128]{3,2,1,0:T(8,128)S(1)}, f32[2,1024,128]{2,...) custom-call(s32[4]{0:T(128)S(1)} %pad_add_fusion.scalars, ...), custom_call_target="tpu_custom_call" | custom-call | flops 62914560 | bytes 12582912 | tf_op jit(solution)/shard_map/second/pallas_call | solution.py:243
  35.6 13.5 %main.5 = (f32[2,4,128,256]{3,2,1,0:T(8,128)S(1)}, bf16[2,4,128,256]{3,2,1,0:T(8,128)(2,1)S(1)}, f32[7,2,1024,128]{3,2,1,0:T(8,128)S(1)}, bf16[2,1024,256]{2,1,0:T(8,128)(2,1)S(1)}, bf16[2,1024,256]{2,1,0:T(8,128)(2,1)S(1)}) custom-call(bf16[2,1024,256]{2,1,0:T(8,128)(2,1)S(1)} %get-tuple-element.46.near, ...), custom_call_target="tpu_custom_call", output_to_operand_aliasing={{2}: (7, {})} | custom-call | flops 10737418240 | bytes 1048576 | tf_op jit(solution)/shard_map/main/pallas_call | solution.py:374
  49.2 13.7 %main.6 = (f32[2,4,128,256]{3,2,1,0:T(8,128)S(1)}, bf16[2,4,128,256]{3,2,1,0:T(8,128)(2,1)S(1)}, f32[7,2,1024,128]{3,2,1,0:T(8,128)S(1)}, bf16[2,1024,256]{2,1,0:T(8,128)(2,1)S(1)}, bf16[2,1024,256]{2,1,0:T(8,128)(2,1)S(1)}) custom-call(bf16[2,1024,256]{2,1,0:T(8,128)(2,1)S(1)} %get-tuple-element.56.near, ...), custom_call_target="tpu_custom_call", output_to_operand_aliasing={{2}: (7, {})} | custom-call | flops 10737418240 | bytes 1048576 | tf_op jit(solution)/shard_map/main/pallas_call | solution.py:374
  62.9 0.6 collective-permute-start.6
  63.6 1.5 %collective-permute-start.5 = (bf16[2,4,64,256]{3,2,1,0:T(8,128)(2,1)S(1)}, bf16[2,4,64,256]{3,2,1,0:T(8,128)(2,1)S(1)}, u32[]{:S(2)}, u32[]{:S(2)}) collective-permute-start(bf16[2,4,64,256]{3,2,1,0:T(8,128)(2,1)S(1)} %slice.127), channel_id=1, source_target_pairs={{0,8},{4,12},{8,0},{12,4},{16,24},{20,28},{24,16},{28,20},{1,9},{5... | collective-permute-start | bytes 786440 | tf_op jit(solution)/shard_map/ppermute | solution.py:44
  65.1 13.5 %main.7 = (f32[2,4,128,256]{3,2,1,0:T(8,128)S(1)}, bf16[2,4,128,256]{3,2,1,0:T(8,128)(2,1)S(1)}, f32[7,2,1024,128]{3,2,1,0:T(8,128)S(1)}, bf16[1,1024,256]{2,1,0:T(8,128)(2,1)S(1)}, bf16[1,1024,256]{2,1,0:T(8,128)(2,1)S(1)}) custom-call(bf16[2,1024,256]{2,1,0:T(8,128)(2,1)S(1)} %get-tuple-element.61.near, ...), custom_call_target="tpu_custom_call", output_to_operand_aliasing={{2}: (7, {})} | custom-call | flops 10737418240 | bytes 1048576 | tf_op jit(solution)/shard_map/main/pallas_call | solution.py:374
  78.9 0.7 collective-permute-start.7
  79.7 7.6 %main.8 = (f32[2,4,128,128]{3,2,1,0:T(8,128)S(1)}, bf16[2,4,128,128]{3,2,1,0:T(8,128)(2,1)S(1)}, f32[7,2,1024,128]{3,2,1,0:T(8,128)S(1)}, bf16[1,1024,256]{2,1,0:T(8,128)(2,1)S(1)}, bf16[1,1024,256]{2,1,0:T(8,128)(2,1)S(1)}) custom-call(bf16[1,1024,256]{2,1,0:T(8,128)(2,1)S(1)} %get-tuple-element.67.near, ...), custom_call_target="tpu_custom_call", output_to_operand_aliasing={{2}: (7, {})} | custom-call | flops 5368709120 | bytes 1048576 | tf_op jit(solution)/shard_map/main/pallas_call | solution.py:374
  87.9 1.0 collective-permute-done.10
  89.0 1.5 %collective-permute-start.11 = (bf16[2,4,64,128]{3,2,1,0:T(8,128)(2,1)S(1)}, bf16[2,4,64,128]{3,2,1,0:T(8,128)(2,1)S(1)}, u32[]{:S(2)}, u32[]{:S(2)}) collective-permute-start(bf16[2,4,64,128]{3,2,1,0:T(8,128)(2,1)S(1)} %slice.131), channel_id=1, source_target_pairs={{0,8},{4,12},{8,0},{12,4},{16,24},{20,28},{24,16},{28,20},{1,9},{5... | collective-permute-start | bytes 393224 | tf_op jit(solution)/shard_map/ppermute | solution.py:44
  90.5 6.9 %main.9 = (f32[2,4,128,128]{3,2,1,0:T(8,128)S(1)}, bf16[2,4,128,128]{3,2,1,0:T(8,128)(2,1)S(1)}, f32[7,2,1024,128]{3,2,1,0:T(8,128)S(1)}) custom-call(bf16[1,1024,256]{2,1,0:T(8,128)(2,1)S(1)} %get-tuple-element.73.near, bf16[1,1024,256]{2,1,0:T(8,128)(2,1)S(1)} %get-tuple-element.74.far, ...), custom_call_target="tpu_custom_call", output_to_operand_aliasing={{2}: (7, {})} | custom-call | flops 5368709120 | bytes 1048576 | tf_op jit(solution)/shard_map/main/pallas_call | solution.py:374
  97.4 3.0 %collective-permute-start.14 = (bf16[2,4,32,256]{3,2,1,0:T(8,128)(2,1)S(1)}, bf16[2,4,32,256]{3,2,1,0:T(8,128)(2,1)S(1)}, u32[]{:S(2)}, u32[]{:S(2)}) collective-permute-start(bf16[2,4,32,256]{3,2,1,0:T(8,128)(2,1)S(1)} %slice.132), channel_id=1, source_target_pairs={{0,16},{4,20},{8,24},{12,28},{16,0},{20,4},{24,8},{28,12},{1,17},{... | collective-permute-start | bytes 393224 | tf_op jit(solution)/shard_map/ppermute | solution.py:44
  100.5 0.6 collective-permute-start.9
  101.1 2.5 %collective-permute-start.17 = (bf16[2,4,32,128]{3,2,1,0:T(8,128)(2,1)S(1)}, bf16[2,4,32,128]{3,2,1,0:T(8,128)(2,1)S(1)}, u32[]{:S(2)}, u32[]{:S(2)}) collective-permute-start(bf16[2,4,32,128]{3,2,1,0:T(8,128)(2,1)S(1)} %slice.134), channel_id=1, source_target_pairs={{0,16},{4,20},{8,24},{12,28},{16,0},{20,4},{24,8},{28,12},{1,17},{... | collective-permute-start | bytes 196616 | tf_op jit(solution)/shard_map/ppermute | solution.py:44
  103.7 1.9 %collective-permute-start.13 = (bf16[2,4,64,128]{3,2,1,0:T(8,128)(2,1)S(1)}, bf16[2,4,64,128]{3,2,1,0:T(8,128)(2,1)S(1)}, u32[]{:S(2)}, u32[]{:S(2)}) collective-permute-start(bf16[2,4,64,128]{3,2,1,0:T(8,128)(2,1)S(1)} %slice.129), channel_id=1, source_target_pairs={{0,8},{4,12},{8,0},{12,4},{16,24},{20,28},{24,16},{28,20},{1,9},{5... | collective-permute-start | bytes 393224 | tf_op jit(solution)/shard_map/ppermute | solution.py:44
  105.6 10.9 %collective-permute-done.9 = bf16[2,4,64,256]{3,2,1,0:T(8,128)(2,1)S(1)} collective-permute-done((bf16[2,4,64,256]{3,2,1,0:T(8,128)(2,1)S(1)}, bf16[2,4,64,256]{3,2,1,0:T(8,128)(2,1)S(1)}, u32[]{:S(2)}, u32[]{:S(2)}) %collective-permute-start.9) | collective-permute-done | bytes 262176 | tf_op jit(solution)/shard_map/ppermute | solution.py:44
  116.8 1.9 %collective-permute-done.13 = bf16[2,4,64,128]{3,2,1,0:T(8,128)(2,1)S(1)} collective-permute-done((bf16[2,4,64,128]{3,2,1,0:T(8,128)(2,1)S(1)}, bf16[2,4,64,128]{3,2,1,0:T(8,128)(2,1)S(1)}, u32[]{:S(2)}, u32[]{:S(2)}) %collective-permute-start.13) | collective-permute-done | bytes 131104 | tf_op jit(solution)/shard_map/ppermute | solution.py:44
  118.8 1.0 collective-permute-start.18
  119.9 5.2 %collective-permute-done.16.refs_7_ = bf16[2,4,32,256]{3,2,1,0:T(8,128)(2,1)S(1)} collective-permute-done((bf16[2,4,32,256]{3,2,1,0:T(8,128)(2,1)S(1)}, bf16[2,4,32,256]{3,2,1,0:T(8,128)(2,1)S(1)}, u32[]{:S(2)}, u32[]{:S(2)}) %collective-permute-start.16) | collective-permute-done | bytes 131104 | tf_op jit(solution)/shard_map/ppermute | solution.py:44
  125.1 0.7 collective-permute-done.18.refs_9_
  125.8 2.5 %covariance.1 = (f32[2,4,32,1024]{3,2,1,0:T(8,128)S(1)}, f32[2,64,128]{2,1,0:T(8,128)S(1)}) custom-call(f32[2,4,32,256]{3,2,1,0:T(8,128)S(1)} %slice.92.refs_0_, f32[2,4,32,256]{3,2,1,0:T(8,128)S(1)} %slice.95.refs_1_, f32[2,4,32,256]{3,2,1,0:T(8,128)S(1)} %slice.98.refs_2_, f32[2,4,32,128]{3,2,1,0:T(8,128)S(1)} %slice.102.refs_3_, ...), custom_call_target="tpu_custom_call" | custom-call | tf_op jit(solution)/shard_map/covariance/pallas_call | solution.py:439
  128.3 2.5 %collective-permute-start.21 = (f32[2,64,128]{2,1,0:T(8,128)S(1)}, f32[2,64,128]{2,1,0:T(8,128)S(1)}, u32[]{:S(2)}, u32[]{:S(2)}) collective-permute-start(f32[2,64,128]{2,1,0:T(8,128)S(1)} %get-tuple-element.79.refs_0_), channel_id=1, source_target_pairs={{0,3},{1,2},{2,1},{3,0},{4,7},{5,6},{6,5},{7,4},{8,11},{9,10},{10,... | collective-permute-start | bytes 196616 | tf_op jit(solution)/shard_map/ppermute | solution.py:44
  131.9 2.1 %collective-permute-done.21.refs_3_ = f32[2,64,128]{2,1,0:T(8,128)S(1)} collective-permute-done((f32[2,64,128]{2,1,0:T(8,128)S(1)}, f32[2,64,128]{2,1,0:T(8,128)S(1)}, u32[]{:S(2)}, u32[]{:S(2)}) %collective-permute-start.21) | collective-permute-done | bytes 65568 | tf_op jit(solution)/shard_map/ppermute | solution.py:44
  134.0 1.1 collective-permute-done.20.refs_2_
  135.6 1.8 %focus.1 = f32[2,128,1024]{2,1,0:T(8,128)} custom-call(f32[2,64,128]{2,1,0:T(8,128)S(1)} %get-tuple-element.79.refs_0_, f32[2,64,128]{2,1,0:T(8,128)S(1)} %collective-permute-done.19.refs_1_, f32[2,64,128]{2,1,0:T(8,128)S(1)} %collective-permute-done.20.refs_2_, f32[2,64,128]{2,1,0:T(8,128)S(1)} %collective-permute-done.21.refs_3_, ...), custom_call_target="tpu_custom_call" | custom-call | tf_op jit(solution)/shard_map/focus/pallas_call | solution.py:503
  (58 shorter events, 3.8 us)
Async XLA Ops:
  0.0 16.3 %collective-permute-start.3 = (bf16[2,1024,1024]{2,1,0:T(8,128)(2,1)}, bf16[2,1024,1024]{2,1,0:T(8,128)(2,1)}, u32[]{:S(2)}, u32[]{:S(2)}) collective-permute-start(bf16[2,1024,1024]{2,1,0:T(8,128)(2,1)} %refs_0_.7), channel_id=1, source_target_pairs={{0,4},{4,0},{8,12},{12,8},{16,20},{20,16},{24,28},{28,24},{1,5},{5... | collective-permute-start | bytes 12582920 | tf_op jit(solution)/shard_map/ppermute | solution.py:44
  0.5 0.9 copy-start.2
  1.4 0.8 copy-start.3
  2.2 0.7 copy-start.4
  3.0 13.3 %collective-permute-start.2 = (f32[16,1024]{1,0:T(8,128)S(1)}, f32[16,1024]{1,0:T(8,128)S(1)}, u32[]{:S(2)}, u32[]{:S(2)}) collective-permute-start(f32[16,1024]{1,0:T(8,128)S(1)} %get-tuple-element.45), channel_id=1, source_target_pairs={{0,24},{4,28},{8,16},{12,20},{16,8},{20,12},{24,0},{28,4},{1,25},{... | collective-permute-start | bytes 196616 | tf_op jit(solution)/shard_map/ppermute | solution.py:44
  7.6 8.7 %collective-permute-start.1 = (f32[16,1024]{1,0:T(8,128)S(1)}, f32[16,1024]{1,0:T(8,128)S(1)}, u32[]{:S(2)}, u32[]{:S(2)}) collective-permute-start(f32[16,1024]{1,0:T(8,128)S(1)} %get-tuple-element.45), channel_id=1, source_target_pairs={{0,16},{4,20},{8,24},{12,28},{16,0},{20,4},{24,8},{28,12},{1,17},{... | collective-permute-start | bytes 196616 | tf_op jit(solution)/shard_map/ppermute | solution.py:44
  7.6 8.7 %collective-permute-start = (f32[24,1024]{1,0:T(8,128)S(1)}, f32[24,1024]{1,0:T(8,128)S(1)}, u32[]{:S(2)}, u32[]{:S(2)}) collective-permute-start(f32[24,1024]{1,0:T(8,128)S(1)} %get-tuple-element.44), channel_id=1, source_target_pairs={{0,8},{4,12},{8,0},{12,4},{16,24},{20,28},{24,16},{28,20},{1,9},{5... | collective-permute-start | bytes 294920 | tf_op jit(solution)/shard_map/ppermute | solution.py:44
  16.3 2.2 %copy-start = (bf16[2,1024,1024]{2,1,0:T(8,128)(2,1)S(1)}, bf16[2,1024,1024]{2,1,0:T(8,128)(2,1)}, u32[]{:S(2)}) copy-start(bf16[2,1024,1024]{2,1,0:T(8,128)(2,1)} %refs_0_.7) | copy-start | bytes 12582916
  18.5 17.1 %copy-start.1 = (bf16[2,1024,1024]{2,1,0:T(8,128)(2,1)S(1)}, bf16[2,1024,1024]{2,1,0:T(8,128)(2,1)}, u32[]{:S(2)}) copy-start(bf16[2,1024,1024]{2,1,0:T(8,128)(2,1)} %refs_0_.7) | copy-start | bytes 12582916
  49.1 14.3 %collective-permute-start.4 = (bf16[2,4,128,256]{3,2,1,0:T(8,128)(2,1)S(1)}, bf16[2,4,128,256]{3,2,1,0:T(8,128)(2,1)S(1)}, u32[]{:S(2)}, u32[]{:S(2)}) collective-permute-start(bf16[2,4,128,256]{3,2,1,0:T(8,128)(2,1)S(1)} %get-tuple-element.55), channel_id=1, source_target_pairs={{0,4},{4,0},{8,12},{12,8},{16,20},{20,16},{24,28},{28,24},{1,5},{5... | collective-permute-start | bytes 1572872 | tf_op jit(solution)/shard_map/ppermute | solution.py:44
  62.9 15.8 %collective-permute-start.6 = (bf16[2,4,128,256]{3,2,1,0:T(8,128)(2,1)S(1)}, bf16[2,4,128,256]{3,2,1,0:T(8,128)(2,1)S(1)}, u32[]{:S(2)}, u32[]{:S(2)}) collective-permute-start(bf16[2,4,128,256]{3,2,1,0:T(8,128)(2,1)S(1)} %get-tuple-element.60), channel_id=1, source_target_pairs={{0,4},{4,0},{8,12},{12,8},{16,20},{20,16},{24,28},{28,24},{1,5},{5... | collective-permute-start | bytes 1572872 | tf_op jit(solution)/shard_map/ppermute | solution.py:44
  63.6 16.0 %collective-permute-start.5 = (bf16[2,4,64,256]{3,2,1,0:T(8,128)(2,1)S(1)}, bf16[2,4,64,256]{3,2,1,0:T(8,128)(2,1)S(1)}, u32[]{:S(2)}, u32[]{:S(2)}) collective-permute-start(bf16[2,4,64,256]{3,2,1,0:T(8,128)(2,1)S(1)} %slice.127), channel_id=1, source_target_pairs={{0,8},{4,12},{8,0},{12,4},{16,24},{20,28},{24,16},{28,20},{1,9},{5... | collective-permute-start | bytes 786440 | tf_op jit(solution)/shard_map/ppermute | solution.py:44
  78.7 9.1 %collective-permute-start.8 = (bf16[2,4,128,256]{3,2,1,0:T(8,128)(2,1)S(1)}, bf16[2,4,128,256]{3,2,1,0:T(8,128)(2,1)S(1)}, u32[]{:S(2)}, u32[]{:S(2)}) collective-permute-start(bf16[2,4,128,256]{3,2,1,0:T(8,128)(2,1)S(1)} %get-tuple-element.66), channel_id=1, source_target_pairs={{0,4},{4,0},{8,12},{12,8},{16,20},{20,16},{24,28},{28,24},{1,5},{5... | collective-permute-start | bytes 1572872 | tf_op jit(solution)/shard_map/ppermute | solution.py:44
  78.9 8.8 %collective-permute-start.7 = (bf16[2,4,64,256]{3,2,1,0:T(8,128)(2,1)S(1)}, bf16[2,4,64,256]{3,2,1,0:T(8,128)(2,1)S(1)}, u32[]{:S(2)}, u32[]{:S(2)}) collective-permute-start(bf16[2,4,64,256]{3,2,1,0:T(8,128)(2,1)S(1)} %slice.126), channel_id=1, source_target_pairs={{0,8},{4,12},{8,0},{12,4},{16,24},{20,28},{24,16},{28,20},{1,9},{5... | collective-permute-start | bytes 786440 | tf_op jit(solution)/shard_map/ppermute | solution.py:44
  87.3 1.6 %collective-permute-start.10 = (bf16[2,4,128,128]{3,2,1,0:T(8,128)(2,1)S(1)}, bf16[2,4,128,128]{3,2,1,0:T(8,128)(2,1)S(1)}, u32[]{:S(2)}, u32[]{:S(2)}) collective-permute-start(bf16[2,4,128,128]{3,2,1,0:T(8,128)(2,1)S(1)} %get-tuple-element.72), channel_id=1, source_target_pairs={{0,4},{4,0},{8,12},{12,8},{16,20},{20,16},{24,28},{28,24},{1,5},{5... | collective-permute-start | bytes 786440 | tf_op jit(solution)/shard_map/ppermute | solution.py:44
  89.0 12.0 %collective-permute-start.11 = (bf16[2,4,64,128]{3,2,1,0:T(8,128)(2,1)S(1)}, bf16[2,4,64,128]{3,2,1,0:T(8,128)(2,1)S(1)}, u32[]{:S(2)}, u32[]{:S(2)}) collective-permute-start(bf16[2,4,64,128]{3,2,1,0:T(8,128)(2,1)S(1)} %slice.131), channel_id=1, source_target_pairs={{0,8},{4,12},{8,0},{12,4},{16,24},{20,28},{24,16},{28,20},{1,9},{5... | collective-permute-start | bytes 393224 | tf_op jit(solution)/shard_map/ppermute | solution.py:44
  97.3 6.3 %collective-permute-start.12 = (bf16[2,4,128,128]{3,2,1,0:T(8,128)(2,1)S(1)}, bf16[2,4,128,128]{3,2,1,0:T(8,128)(2,1)S(1)}, u32[]{:S(2)}, u32[]{:S(2)}) collective-permute-start(bf16[2,4,128,128]{3,2,1,0:T(8,128)(2,1)S(1)} %get-tuple-element.78), channel_id=1, source_target_pairs={{0,4},{4,0},{8,12},{12,8},{16,20},{20,16},{24,28},{28,24},{1,5},{5... | collective-permute-start | bytes 786440 | tf_op jit(solution)/shard_map/ppermute | solution.py:44
  97.4 22.5 %collective-permute-start.14 = (bf16[2,4,32,256]{3,2,1,0:T(8,128)(2,1)S(1)}, bf16[2,4,32,256]{3,2,1,0:T(8,128)(2,1)S(1)}, u32[]{:S(2)}, u32[]{:S(2)}) collective-permute-start(bf16[2,4,32,256]{3,2,1,0:T(8,128)(2,1)S(1)} %slice.132), channel_id=1, source_target_pairs={{0,16},{4,20},{8,24},{12,28},{16,0},{20,4},{24,8},{28,12},{1,17},{... | collective-permute-start | bytes 393224 | tf_op jit(solution)/shard_map/ppermute | solution.py:44
  100.4 19.5 %collective-permute-start.15 = (bf16[2,4,32,256]{3,2,1,0:T(8,128)(2,1)S(1)}, bf16[2,4,32,256]{3,2,1,0:T(8,128)(2,1)S(1)}, u32[]{:S(2)}, u32[]{:S(2)}) collective-permute-start(bf16[2,4,32,256]{3,2,1,0:T(8,128)(2,1)S(1)} %slice.130), channel_id=1, source_target_pairs={{0,16},{4,20},{8,24},{12,28},{16,0},{20,4},{24,8},{28,12},{1,17},{... | collective-permute-start | bytes 393224 | tf_op jit(solution)/shard_map/ppermute | solution.py:44
  100.5 16.1 %collective-permute-start.9 = (bf16[2,4,64,256]{3,2,1,0:T(8,128)(2,1)S(1)}, bf16[2,4,64,256]{3,2,1,0:T(8,128)(2,1)S(1)}, u32[]{:S(2)}, u32[]{:S(2)}) collective-permute-start(bf16[2,4,64,256]{3,2,1,0:T(8,128)(2,1)S(1)} %slice.125), channel_id=1, source_target_pairs={{0,8},{4,12},{8,0},{12,4},{16,24},{20,28},{24,16},{28,20},{1,9},{5... | collective-permute-start | bytes 786440 | tf_op jit(solution)/shard_map/ppermute | solution.py:44
  101.1 18.8 %collective-permute-start.17 = (bf16[2,4,32,128]{3,2,1,0:T(8,128)(2,1)S(1)}, bf16[2,4,32,128]{3,2,1,0:T(8,128)(2,1)S(1)}, u32[]{:S(2)}, u32[]{:S(2)}) collective-permute-start(bf16[2,4,32,128]{3,2,1,0:T(8,128)(2,1)S(1)} %slice.134), channel_id=1, source_target_pairs={{0,16},{4,20},{8,24},{12,28},{16,0},{20,4},{24,8},{28,12},{1,17},{... | collective-permute-start | bytes 196616 | tf_op jit(solution)/shard_map/ppermute | solution.py:44
  103.7 15.0 %collective-permute-start.13 = (bf16[2,4,64,128]{3,2,1,0:T(8,128)(2,1)S(1)}, bf16[2,4,64,128]{3,2,1,0:T(8,128)(2,1)S(1)}, u32[]{:S(2)}, u32[]{:S(2)}) collective-permute-start(bf16[2,4,64,128]{3,2,1,0:T(8,128)(2,1)S(1)} %slice.129), channel_id=1, source_target_pairs={{0,8},{4,12},{8,0},{12,4},{16,24},{20,28},{24,16},{28,20},{1,9},{5... | collective-permute-start | bytes 393224 | tf_op jit(solution)/shard_map/ppermute | solution.py:44
  116.7 8.4 %collective-permute-start.16 = (bf16[2,4,32,256]{3,2,1,0:T(8,128)(2,1)S(1)}, bf16[2,4,32,256]{3,2,1,0:T(8,128)(2,1)S(1)}, u32[]{:S(2)}, u32[]{:S(2)}) collective-permute-start(bf16[2,4,32,256]{3,2,1,0:T(8,128)(2,1)S(1)} %slice.128), channel_id=1, source_target_pairs={{0,16},{4,20},{8,24},{12,28},{16,0},{20,4},{24,8},{28,12},{1,17},{... | collective-permute-start | bytes 393224 | tf_op jit(solution)/shard_map/ppermute | solution.py:44
  118.8 7.1 %collective-permute-start.18 = (bf16[2,4,32,128]{3,2,1,0:T(8,128)(2,1)S(1)}, bf16[2,4,32,128]{3,2,1,0:T(8,128)(2,1)S(1)}, u32[]{:S(2)}, u32[]{:S(2)}) collective-permute-start(bf16[2,4,32,128]{3,2,1,0:T(8,128)(2,1)S(1)} %slice.133), channel_id=1, source_target_pairs={{0,16},{4,20},{8,24},{12,28},{16,0},{20,4},{24,8},{28,12},{1,17},{... | collective-permute-start | bytes 196616 | tf_op jit(solution)/shard_map/ppermute | solution.py:44
  128.3 5.7 %collective-permute-start.21 = (f32[2,64,128]{2,1,0:T(8,128)S(1)}, f32[2,64,128]{2,1,0:T(8,128)S(1)}, u32[]{:S(2)}, u32[]{:S(2)}) collective-permute-start(f32[2,64,128]{2,1,0:T(8,128)S(1)} %get-tuple-element.79.refs_0_), channel_id=1, source_target_pairs={{0,3},{1,2},{2,1},{3,0},{4,7},{5,6},{6,5},{7,4},{8,11},{9,10},{10,... | collective-permute-start | bytes 196616 | tf_op jit(solution)/shard_map/ppermute | solution.py:44
  130.8 4.3 %collective-permute-start.20 = (f32[2,64,128]{2,1,0:T(8,128)S(1)}, f32[2,64,128]{2,1,0:T(8,128)S(1)}, u32[]{:S(2)}, u32[]{:S(2)}) collective-permute-start(f32[2,64,128]{2,1,0:T(8,128)S(1)} %get-tuple-element.79.refs_0_), channel_id=1, source_target_pairs={{0,2},{1,3},{2,0},{3,1},{4,6},{5,7},{6,4},{7,5},{8,10},{9,11},{10,... | collective-permute-start | bytes 196616 | tf_op jit(solution)/shard_map/ppermute | solution.py:44
  131.3 4.3 %collective-permute-start.19 = (f32[2,64,128]{2,1,0:T(8,128)S(1)}, f32[2,64,128]{2,1,0:T(8,128)S(1)}, u32[]{:S(2)}, u32[]{:S(2)}) collective-permute-start(f32[2,64,128]{2,1,0:T(8,128)S(1)} %get-tuple-element.79.refs_0_), channel_id=1, source_target_pairs={{0,1},{1,0},{2,3},{3,2},{4,5},{5,4},{6,7},{7,6},{8,9},{9,8},{10,11... | collective-permute-start | bytes 196616 | tf_op jit(solution)/shard_map/ppermute | solution.py:44

commit v2 on v1

--- a/solution.py
+++ b/solution.py
@@ -166,7 +166,7 @@
         scratch_shapes=[pltpu.VMEM((beams, LANES), F32), pltpu.VMEM((LANES, beams), F32)],
         compiler_params=pltpu.CompilerParams(vmem_limit_bytes=SMALL_LIMIT * MIB),
         cost_estimate=pl.CostEstimate(
-            flops=30 * beams * beams, bytes_accessed=8 * beams * beams, transcendentals=0
+            flops=4000 * beams * beams, bytes_accessed=8 * beams * beams, transcendentals=0
         ),
         name="first",
     )(scalars, mine)
@@ -233,7 +233,7 @@
         step[1, at, :] = sine
         return 0
 
-    lax.fori_loop(0, beams // 16, part, 0)
+    lax.fori_loop(0, beams // 16, part, 0, unroll=2)
     for copy in copies:
         copy.wait()
 
@@ -260,7 +260,7 @@
         ],
         compiler_params=pltpu.CompilerParams(vmem_limit_bytes=SMALL_LIMIT * MIB),
         cost_estimate=pl.CostEstimate(
-            flops=60 * beams * beams, bytes_accessed=12 * beams * beams, transcendentals=0
+            flops=8000 * beams * beams, bytes_accessed=12 * beams * beams, transcendentals=0
         ),
         name="second",
     )(scalars, mine, near, middle, far, pulse_data, other)
@@ -284,7 +284,7 @@
 
 
 def main_limit(classes):
-    return (8 if classes <= 4 else 40) * MIB
+    return (7 if classes <= 4 else 40) * MIB
 
 
 def main_kernel(

time: 138 us -> 133 us (0.964)
  Pallas kernels: 84.7 us -> 82.2 us
  local copies, waits for them, and re-layouts: 4.87 us -> 2.69 us
    pallas_call x1, Pallas kernels: 17.1 us -> 14.6 us  [second_tables(): pl.pallas_call(functools.partial(second_kernel, ranges), in_specs=[SMEM]...]
    unnamed x10 -> x8, local copies, waits for them, and re-layouts: 4.59 us -> 2.41 us
  transfers between devices with their start and end apart: 22 -> 22, of which waited for: 9 -> 8; matrix products, arithmetic and copies ran while one was open for 1% -> 1% of each run, Pallas kernels for 36% -> 37%
where the time goes in v2:
time: 133 us
  Pallas kernels  82.2 us (62%)
  waiting for transfers between devices  23.6 us (18%)
  starting transfers between devices  23.2 us (17%)
  local copies, waits for them, and re-layouts  2.69 us (2%)
    pallas_call x5, Pallas kernels, partial_spectrum(): pl.pallas_call(functools.partial(main_kernel, start, classes, chunks > 0)...  55.2 us
    ppermute x22, waiting for transfers between devices, swap(): return lax.ppermute(block, axis, [(i, i ^ distance) for i in range(count)])  23.6 us
    ppermute x22, starting transfers between devices, swap(): return lax.ppermute(block, axis, [(i, i ^ distance) for i in range(count)])  23.2 us
    pallas_call x1, Pallas kernels, second_tables(): pl.pallas_call(functools.partial(second_kernel, ranges), in_specs=[SMEM]...  14.6 us
    pallas_call x1, Pallas kernels, first_tables(): pl.pallas_call(functools.partial(first_kernel, pulses), in_specs=[SMEM, V...  7.95 us
  transfers between devices with their start and end apart: 22, of which 8 were waited for; matrix products, arithmetic and copies ran while one was open for 1% of the time, Pallas kernels for 37%

profile of v2, /device:TPU:0, one launch (start us, length us, event | category | flops | bytes accessed | tf_op | source)
XLA Modules:
  0.0 132.8 jit_solution(13989496143059770635)
XLA Ops:
  0.5 0.9 copy-done.1
  1.4 0.8 copy-done.2
  2.2 0.7 copy-done.3
  3.0 4.7 %collective-permute-start.2 = (f32[16,1024]{1,0:T(8,128)S(1)}, f32[16,1024]{1,0:T(8,128)S(1)}, u32[]{:S(2)}, u32[]{:S(2)}) collective-permute-start(f32[16,1024]{1,0:T(8,128)S(1)} %get-tuple-element.45), channel_id=1, source_target_pairs={{0,24},{4,28},{8,16},{12,20},{16,8},{20,12},{24,0},{28,4},{1,25},{... | collective-permute-start | bytes 196616 | tf_op jit(solution)/shard_map/ppermute | solution.py:44
  7.6 0.6 collective-permute-start
  8.3 7.9 %first.1 = (bf16[2,1024,1024]{2,1,0:T(8,128)(2,1)S(1)}, bf16[2048,1024]{1,0:T(8,128)(2,1)S(1)}) custom-call(s32[4]{0:T(128)S(1)} %pad_add_fusion.scalars, f32[40,1024]{1,0:T(8,128)S(1)} %get-tuple-element.43.mine), custom_call_target="tpu_custom_call" | custom-call | flops 4194304000 | bytes 8388608 | tf_op jit(solution)/shard_map/first/pallas_call | solution.py:158
  16.3 14.6 %second.1 = (bf16[2,1024,1024]{2,1,0:T(8,128)(2,1)S(1)}, bf16[4,1024,1024]{2,1,0:T(8,128)(2,1)S(1)}, f32[7,2,1024,128]{3,2,1,0:T(8,128)S(1)}, f32[2,1024,128]{2,...) custom-call(s32[4]{0:T(128)S(1)} %pad_add_fusion.scalars, ...), custom_call_target="tpu_custom_call" | custom-call | flops 8388608000 | bytes 12582912 | tf_op jit(solution)/shard_map/second/pallas_call | solution.py:243
  30.9 13.5 %main.5 = (f32[2,4,128,256]{3,2,1,0:T(8,128)S(1)}, bf16[2,4,128,256]{3,2,1,0:T(8,128)(2,1)S(1)}, f32[7,2,1024,128]{3,2,1,0:T(8,128)S(1)}, bf16[2,1024,256]{2,1,0:T(8,128)(2,1)S(1)}, bf16[2,1024,256]{2,1,0:T(8,128)(2,1)S(1)}) custom-call(bf16[2,1024,256]{2,1,0:T(8,128)(2,1)S(1)} %get-tuple-element.46.near, ...), custom_call_target="tpu_custom_call", output_to_operand_aliasing={{2}: (7, {})} | custom-call | flops 10737418240 | bytes 1048576 | tf_op jit(solution)/shard_map/main/pallas_call | solution.py:374
  44.6 13.7 %main.6 = (f32[2,4,128,256]{3,2,1,0:T(8,128)S(1)}, bf16[2,4,128,256]{3,2,1,0:T(8,128)(2,1)S(1)}, f32[7,2,1024,128]{3,2,1,0:T(8,128)S(1)}, bf16[2,1024,256]{2,1,0:T(8,128)(2,1)S(1)}, bf16[2,1024,256]{2,1,0:T(8,128)(2,1)S(1)}) custom-call(bf16[2,1024,256]{2,1,0:T(8,128)(2,1)S(1)} %get-tuple-element.56.near, ...), custom_call_target="tpu_custom_call", output_to_operand_aliasing={{2}: (7, {})} | custom-call | flops 10737418240 | bytes 1048576 | tf_op jit(solution)/shard_map/main/pallas_call | solution.py:374
  58.3 0.6 collective-permute-start.6
  59.0 1.5 %collective-permute-start.5 = (bf16[2,4,64,256]{3,2,1,0:T(8,128)(2,1)S(1)}, bf16[2,4,64,256]{3,2,1,0:T(8,128)(2,1)S(1)}, u32[]{:S(2)}, u32[]{:S(2)}) collective-permute-start(bf16[2,4,64,256]{3,2,1,0:T(8,128)(2,1)S(1)} %slice.127), channel_id=1, source_target_pairs={{0,8},{4,12},{8,0},{12,4},{16,24},{20,28},{24,16},{28,20},{1,9},{5... | collective-permute-start | bytes 786440 | tf_op jit(solution)/shard_map/ppermute | solution.py:44
  60.4 13.5 %main.7 = (f32[2,4,128,256]{3,2,1,0:T(8,128)S(1)}, bf16[2,4,128,256]{3,2,1,0:T(8,128)(2,1)S(1)}, f32[7,2,1024,128]{3,2,1,0:T(8,128)S(1)}, bf16[1,1024,256]{2,1,0:T(8,128)(2,1)S(1)}, bf16[1,1024,256]{2,1,0:T(8,128)(2,1)S(1)}) custom-call(bf16[2,1024,256]{2,1,0:T(8,128)(2,1)S(1)} %get-tuple-element.61.near, ...), custom_call_target="tpu_custom_call", output_to_operand_aliasing={{2}: (7, {})} | custom-call | flops 10737418240 | bytes 1048576 | tf_op jit(solution)/shard_map/main/pallas_call | solution.py:374
  74.2 0.7 collective-permute-start.7
  75.0 7.6 %main.8 = (f32[2,4,128,128]{3,2,1,0:T(8,128)S(1)}, bf16[2,4,128,128]{3,2,1,0:T(8,128)(2,1)S(1)}, f32[7,2,1024,128]{3,2,1,0:T(8,128)S(1)}, bf16[1,1024,256]{2,1,0:T(8,128)(2,1)S(1)}, bf16[1,1024,256]{2,1,0:T(8,128)(2,1)S(1)}) custom-call(bf16[1,1024,256]{2,1,0:T(8,128)(2,1)S(1)} %get-tuple-element.67.near, ...), custom_call_target="tpu_custom_call", output_to_operand_aliasing={{2}: (7, {})} | custom-call | flops 5368709120 | bytes 1048576 | tf_op jit(solution)/shard_map/main/pallas_call | solution.py:374
  83.3 1.0 collective-permute-done.10
  84.4 1.5 %collective-permute-start.11 = (bf16[2,4,64,128]{3,2,1,0:T(8,128)(2,1)S(1)}, bf16[2,4,64,128]{3,2,1,0:T(8,128)(2,1)S(1)}, u32[]{:S(2)}, u32[]{:S(2)}) collective-permute-start(bf16[2,4,64,128]{3,2,1,0:T(8,128)(2,1)S(1)} %slice.131), channel_id=1, source_target_pairs={{0,8},{4,12},{8,0},{12,4},{16,24},{20,28},{24,16},{28,20},{1,9},{5... | collective-permute-start | bytes 393224 | tf_op jit(solution)/shard_map/ppermute | solution.py:44
  85.8 6.8 %main.9 = (f32[2,4,128,128]{3,2,1,0:T(8,128)S(1)}, bf16[2,4,128,128]{3,2,1,0:T(8,128)(2,1)S(1)}, f32[7,2,1024,128]{3,2,1,0:T(8,128)S(1)}) custom-call(bf16[1,1024,256]{2,1,0:T(8,128)(2,1)S(1)} %get-tuple-element.73.near, bf16[1,1024,256]{2,1,0:T(8,128)(2,1)S(1)} %get-tuple-element.74.far, ...), custom_call_target="tpu_custom_call", output_to_operand_aliasing={{2}: (7, {})} | custom-call | flops 5368709120 | bytes 1048576 | tf_op jit(solution)/shard_map/main/pallas_call | solution.py:374
  92.7 3.0 %collective-permute-start.14 = (bf16[2,4,32,256]{3,2,1,0:T(8,128)(2,1)S(1)}, bf16[2,4,32,256]{3,2,1,0:T(8,128)(2,1)S(1)}, u32[]{:S(2)}, u32[]{:S(2)}) collective-permute-start(bf16[2,4,32,256]{3,2,1,0:T(8,128)(2,1)S(1)} %slice.132), channel_id=1, source_target_pairs={{0,16},{4,20},{8,24},{12,28},{16,0},{20,4},{24,8},{28,12},{1,17},{... | collective-permute-start | bytes 393224 | tf_op jit(solution)/shard_map/ppermute | solution.py:44
  95.8 0.6 collective-permute-start.9
  96.4 2.5 %collective-permute-start.17 = (bf16[2,4,32,128]{3,2,1,0:T(8,128)(2,1)S(1)}, bf16[2,4,32,128]{3,2,1,0:T(8,128)(2,1)S(1)}, u32[]{:S(2)}, u32[]{:S(2)}) collective-permute-start(bf16[2,4,32,128]{3,2,1,0:T(8,128)(2,1)S(1)} %slice.134), channel_id=1, source_target_pairs={{0,16},{4,20},{8,24},{12,28},{16,0},{20,4},{24,8},{28,12},{1,17},{... | collective-permute-start | bytes 196616 | tf_op jit(solution)/shard_map/ppermute | solution.py:44
  99.0 1.9 %collective-permute-start.13 = (bf16[2,4,64,128]{3,2,1,0:T(8,128)(2,1)S(1)}, bf16[2,4,64,128]{3,2,1,0:T(8,128)(2,1)S(1)}, u32[]{:S(2)}, u32[]{:S(2)}) collective-permute-start(bf16[2,4,64,128]{3,2,1,0:T(8,128)(2,1)S(1)} %slice.129), channel_id=1, source_target_pairs={{0,8},{4,12},{8,0},{12,4},{16,24},{20,28},{24,16},{28,20},{1,9},{5... | collective-permute-start | bytes 393224 | tf_op jit(solution)/shard_map/ppermute | solution.py:44
  101.0 11.0 %collective-permute-done.9 = bf16[2,4,64,256]{3,2,1,0:T(8,128)(2,1)S(1)} collective-permute-done((bf16[2,4,64,256]{3,2,1,0:T(8,128)(2,1)S(1)}, bf16[2,4,64,256]{3,2,1,0:T(8,128)(2,1)S(1)}, u32[]{:S(2)}, u32[]{:S(2)}) %collective-permute-start.9) | collective-permute-done | bytes 262176 | tf_op jit(solution)/shard_map/ppermute | solution.py:44
  112.1 1.9 %collective-permute-done.13 = bf16[2,4,64,128]{3,2,1,0:T(8,128)(2,1)S(1)} collective-permute-done((bf16[2,4,64,128]{3,2,1,0:T(8,128)(2,1)S(1)}, bf16[2,4,64,128]{3,2,1,0:T(8,128)(2,1)S(1)}, u32[]{:S(2)}, u32[]{:S(2)}) %collective-permute-start.13) | collective-permute-done | bytes 131104 | tf_op jit(solution)/shard_map/ppermute | solution.py:44
  114.1 1.0 collective-permute-start.18
  115.2 5.2 %collective-permute-done.16.refs_7_ = bf16[2,4,32,256]{3,2,1,0:T(8,128)(2,1)S(1)} collective-permute-done((bf16[2,4,32,256]{3,2,1,0:T(8,128)(2,1)S(1)}, bf16[2,4,32,256]{3,2,1,0:T(8,128)(2,1)S(1)}, u32[]{:S(2)}, u32[]{:S(2)}) %collective-permute-start.16) | collective-permute-done | bytes 131104 | tf_op jit(solution)/shard_map/ppermute | solution.py:44
  120.4 0.7 collective-permute-done.18.refs_9_
  121.1 2.5 %covariance.1 = (f32[2,4,32,1024]{3,2,1,0:T(8,128)S(1)}, f32[2,64,128]{2,1,0:T(8,128)S(1)}) custom-call(f32[2,4,32,256]{3,2,1,0:T(8,128)S(1)} %slice.92.refs_0_, f32[2,4,32,256]{3,2,1,0:T(8,128)S(1)} %slice.95.refs_1_, f32[2,4,32,256]{3,2,1,0:T(8,128)S(1)} %slice.98.refs_2_, f32[2,4,32,128]{3,2,1,0:T(8,128)S(1)} %slice.102.refs_3_, ...), custom_call_target="tpu_custom_call" | custom-call | tf_op jit(solution)/shard_map/covariance/pallas_call | solution.py:439
  123.6 2.5 %collective-permute-start.21 = (f32[2,64,128]{2,1,0:T(8,128)S(1)}, f32[2,64,128]{2,1,0:T(8,128)S(1)}, u32[]{:S(2)}, u32[]{:S(2)}) collective-permute-start(f32[2,64,128]{2,1,0:T(8,128)S(1)} %get-tuple-element.79.refs_0_), channel_id=1, source_target_pairs={{0,3},{1,2},{2,1},{3,0},{4,7},{5,6},{6,5},{7,4},{8,11},{9,10},{10,... | collective-permute-start | bytes 196616 | tf_op jit(solution)/shard_map/ppermute | solution.py:44
  126.7 0.5 collective-permute-start.19
  127.2 2.1 %collective-permute-done.21.refs_3_ = f32[2,64,128]{2,1,0:T(8,128)S(1)} collective-permute-done((f32[2,64,128]{2,1,0:T(8,128)S(1)}, f32[2,64,128]{2,1,0:T(8,128)S(1)}, u32[]{:S(2)}, u32[]{:S(2)}) %collective-permute-start.21) | collective-permute-done | bytes 65568 | tf_op jit(solution)/shard_map/ppermute | solution.py:44
  129.3 1.1 collective-permute-done.20.refs_2_
  130.9 1.8 %focus.1 = f32[2,128,1024]{2,1,0:T(8,128)} custom-call(f32[2,64,128]{2,1,0:T(8,128)S(1)} %get-tuple-element.79.refs_0_, f32[2,64,128]{2,1,0:T(8,128)S(1)} %collective-permute-done.19.refs_1_, f32[2,64,128]{2,1,0:T(8,128)S(1)} %collective-permute-done.20.refs_2_, f32[2,64,128]{2,1,0:T(8,128)S(1)} %collective-permute-done.21.refs_3_, ...), custom_call_target="tpu_custom_call" | custom-call | tf_op jit(solution)/shard_map/focus/pallas_call | solution.py:503
  (56 shorter events, 3.3 us)
Async XLA Ops:
  0.0 16.3 %collective-permute-start.3 = (bf16[2,1024,1024]{2,1,0:T(8,128)(2,1)}, bf16[2,1024,1024]{2,1,0:T(8,128)(2,1)}, u32[]{:S(2)}, u32[]{:S(2)}) collective-permute-start(bf16[2,1024,1024]{2,1,0:T(8,128)(2,1)} %refs_0_.7), channel_id=1, source_target_pairs={{0,4},{4,0},{8,12},{12,8},{16,20},{20,16},{24,28},{28,24},{1,5},{5... | collective-permute-start | bytes 12582920 | tf_op jit(solution)/shard_map/ppermute | solution.py:44
  0.5 0.9 copy-start.1
  1.4 0.8 copy-start.2
  2.2 0.7 copy-start.3
  3.0 13.3 %collective-permute-start.2 = (f32[16,1024]{1,0:T(8,128)S(1)}, f32[16,1024]{1,0:T(8,128)S(1)}, u32[]{:S(2)}, u32[]{:S(2)}) collective-permute-start(f32[16,1024]{1,0:T(8,128)S(1)} %get-tuple-element.45), channel_id=1, source_target_pairs={{0,24},{4,28},{8,16},{12,20},{16,8},{20,12},{24,0},{28,4},{1,25},{... | collective-permute-start | bytes 196616 | tf_op jit(solution)/shard_map/ppermute | solution.py:44
  7.6 8.7 %collective-permute-start.1 = (f32[16,1024]{1,0:T(8,128)S(1)}, f32[16,1024]{1,0:T(8,128)S(1)}, u32[]{:S(2)}, u32[]{:S(2)}) collective-permute-start(f32[16,1024]{1,0:T(8,128)S(1)} %get-tuple-element.45), channel_id=1, source_target_pairs={{0,16},{4,20},{8,24},{12,28},{16,0},{20,4},{24,8},{28,12},{1,17},{... | collective-permute-start | bytes 196616 | tf_op jit(solution)/shard_map/ppermute | solution.py:44
  7.6 8.7 %collective-permute-start = (f32[24,1024]{1,0:T(8,128)S(1)}, f32[24,1024]{1,0:T(8,128)S(1)}, u32[]{:S(2)}, u32[]{:S(2)}) collective-permute-start(f32[24,1024]{1,0:T(8,128)S(1)} %get-tuple-element.44), channel_id=1, source_target_pairs={{0,8},{4,12},{8,0},{12,4},{16,24},{20,28},{24,16},{28,20},{1,9},{5... | collective-permute-start | bytes 294920 | tf_op jit(solution)/shard_map/ppermute | solution.py:44
  8.3 8.0 %copy-start = (bf16[2,1024,1024]{2,1,0:T(8,128)(2,1)S(1)}, bf16[2,1024,1024]{2,1,0:T(8,128)(2,1)}, u32[]{:S(2)}) copy-start(bf16[2,1024,1024]{2,1,0:T(8,128)(2,1)} %refs_0_.7) | copy-start | bytes 12582916
  44.5 14.3 %collective-permute-start.4 = (bf16[2,4,128,256]{3,2,1,0:T(8,128)(2,1)S(1)}, bf16[2,4,128,256]{3,2,1,0:T(8,128)(2,1)S(1)}, u32[]{:S(2)}, u32[]{:S(2)}) collective-permute-start(bf16[2,4,128,256]{3,2,1,0:T(8,128)(2,1)S(1)} %get-tuple-element.55), channel_id=1, source_target_pairs={{0,4},{4,0},{8,12},{12,8},{16,20},{20,16},{24,28},{28,24},{1,5},{5... | collective-permute-start | bytes 1572872 | tf_op jit(solution)/shard_map/ppermute | solution.py:44
  58.3 15.8 %collective-permute-start.6 = (bf16[2,4,128,256]{3,2,1,0:T(8,128)(2,1)S(1)}, bf16[2,4,128,256]{3,2,1,0:T(8,128)(2,1)S(1)}, u32[]{:S(2)}, u32[]{:S(2)}) collective-permute-start(bf16[2,4,128,256]{3,2,1,0:T(8,128)(2,1)S(1)} %get-tuple-element.60), channel_id=1, source_target_pairs={{0,4},{4,0},{8,12},{12,8},{16,20},{20,16},{24,28},{28,24},{1,5},{5... | collective-permute-start | bytes 1572872 | tf_op jit(solution)/shard_map/ppermute | solution.py:44
  59.0 16.0 %collective-permute-start.5 = (bf16[2,4,64,256]{3,2,1,0:T(8,128)(2,1)S(1)}, bf16[2,4,64,256]{3,2,1,0:T(8,128)(2,1)S(1)}, u32[]{:S(2)}, u32[]{:S(2)}) collective-permute-start(bf16[2,4,64,256]{3,2,1,0:T(8,128)(2,1)S(1)} %slice.127), channel_id=1, source_target_pairs={{0,8},{4,12},{8,0},{12,4},{16,24},{20,28},{24,16},{28,20},{1,9},{5... | collective-permute-start | bytes 786440 | tf_op jit(solution)/shard_map/ppermute | solution.py:44
  74.0 9.1 %collective-permute-start.8 = (bf16[2,4,128,256]{3,2,1,0:T(8,128)(2,1)S(1)}, bf16[2,4,128,256]{3,2,1,0:T(8,128)(2,1)S(1)}, u32[]{:S(2)}, u32[]{:S(2)}) collective-permute-start(bf16[2,4,128,256]{3,2,1,0:T(8,128)(2,1)S(1)} %get-tuple-element.66), channel_id=1, source_target_pairs={{0,4},{4,0},{8,12},{12,8},{16,20},{20,16},{24,28},{28,24},{1,5},{5... | collective-permute-start | bytes 1572872 | tf_op jit(solution)/shard_map/ppermute | solution.py:44
  74.2 8.8 %collective-permute-start.7 = (bf16[2,4,64,256]{3,2,1,0:T(8,128)(2,1)S(1)}, bf16[2,4,64,256]{3,2,1,0:T(8,128)(2,1)S(1)}, u32[]{:S(2)}, u32[]{:S(2)}) collective-permute-start(bf16[2,4,64,256]{3,2,1,0:T(8,128)(2,1)S(1)} %slice.126), channel_id=1, source_target_pairs={{0,8},{4,12},{8,0},{12,4},{16,24},{20,28},{24,16},{28,20},{1,9},{5... | collective-permute-start | bytes 786440 | tf_op jit(solution)/shard_map/ppermute | solution.py:44
  82.7 1.6 %collective-permute-start.10 = (bf16[2,4,128,128]{3,2,1,0:T(8,128)(2,1)S(1)}, bf16[2,4,128,128]{3,2,1,0:T(8,128)(2,1)S(1)}, u32[]{:S(2)}, u32[]{:S(2)}) collective-permute-start(bf16[2,4,128,128]{3,2,1,0:T(8,128)(2,1)S(1)} %get-tuple-element.72), channel_id=1, source_target_pairs={{0,4},{4,0},{8,12},{12,8},{16,20},{20,16},{24,28},{28,24},{1,5},{5... | collective-permute-start | bytes 786440 | tf_op jit(solution)/shard_map/ppermute | solution.py:44
  84.4 12.0 %collective-permute-start.11 = (bf16[2,4,64,128]{3,2,1,0:T(8,128)(2,1)S(1)}, bf16[2,4,64,128]{3,2,1,0:T(8,128)(2,1)S(1)}, u32[]{:S(2)}, u32[]{:S(2)}) collective-permute-start(bf16[2,4,64,128]{3,2,1,0:T(8,128)(2,1)S(1)} %slice.131), channel_id=1, source_target_pairs={{0,8},{4,12},{8,0},{12,4},{16,24},{20,28},{24,16},{28,20},{1,9},{5... | collective-permute-start | bytes 393224 | tf_op jit(solution)/shard_map/ppermute | solution.py:44
  92.7 6.3 %collective-permute-start.12 = (bf16[2,4,128,128]{3,2,1,0:T(8,128)(2,1)S(1)}, bf16[2,4,128,128]{3,2,1,0:T(8,128)(2,1)S(1)}, u32[]{:S(2)}, u32[]{:S(2)}) collective-permute-start(bf16[2,4,128,128]{3,2,1,0:T(8,128)(2,1)S(1)} %get-tuple-element.78), channel_id=1, source_target_pairs={{0,4},{4,0},{8,12},{12,8},{16,20},{20,16},{24,28},{28,24},{1,5},{5... | collective-permute-start | bytes 786440 | tf_op jit(solution)/shard_map/ppermute | solution.py:44
  92.7 22.5 %collective-permute-start.14 = (bf16[2,4,32,256]{3,2,1,0:T(8,128)(2,1)S(1)}, bf16[2,4,32,256]{3,2,1,0:T(8,128)(2,1)S(1)}, u32[]{:S(2)}, u32[]{:S(2)}) collective-permute-start(bf16[2,4,32,256]{3,2,1,0:T(8,128)(2,1)S(1)} %slice.132), channel_id=1, source_target_pairs={{0,16},{4,20},{8,24},{12,28},{16,0},{20,4},{24,8},{28,12},{1,17},{... | collective-permute-start | bytes 393224 | tf_op jit(solution)/shard_map/ppermute | solution.py:44
  95.7 19.5 %collective-permute-start.15 = (bf16[2,4,32,256]{3,2,1,0:T(8,128)(2,1)S(1)}, bf16[2,4,32,256]{3,2,1,0:T(8,128)(2,1)S(1)}, u32[]{:S(2)}, u32[]{:S(2)}) collective-permute-start(bf16[2,4,32,256]{3,2,1,0:T(8,128)(2,1)S(1)} %slice.130), channel_id=1, source_target_pairs={{0,16},{4,20},{8,24},{12,28},{16,0},{20,4},{24,8},{28,12},{1,17},{... | collective-permute-start | bytes 393224 | tf_op jit(solution)/shard_map/ppermute | solution.py:44
  95.8 16.1 %collective-permute-start.9 = (bf16[2,4,64,256]{3,2,1,0:T(8,128)(2,1)S(1)}, bf16[2,4,64,256]{3,2,1,0:T(8,128)(2,1)S(1)}, u32[]{:S(2)}, u32[]{:S(2)}) collective-permute-start(bf16[2,4,64,256]{3,2,1,0:T(8,128)(2,1)S(1)} %slice.125), channel_id=1, source_target_pairs={{0,8},{4,12},{8,0},{12,4},{16,24},{20,28},{24,16},{28,20},{1,9},{5... | collective-permute-start | bytes 786440 | tf_op jit(solution)/shard_map/ppermute | solution.py:44
  96.4 18.8 %collective-permute-start.17 = (bf16[2,4,32,128]{3,2,1,0:T(8,128)(2,1)S(1)}, bf16[2,4,32,128]{3,2,1,0:T(8,128)(2,1)S(1)}, u32[]{:S(2)}, u32[]{:S(2)}) collective-permute-start(bf16[2,4,32,128]{3,2,1,0:T(8,128)(2,1)S(1)} %slice.134), channel_id=1, source_target_pairs={{0,16},{4,20},{8,24},{12,28},{16,0},{20,4},{24,8},{28,12},{1,17},{... | collective-permute-start | bytes 196616 | tf_op jit(solution)/shard_map/ppermute | solution.py:44
  99.0 15.0 %collective-permute-start.13 = (bf16[2,4,64,128]{3,2,1,0:T(8,128)(2,1)S(1)}, bf16[2,4,64,128]{3,2,1,0:T(8,128)(2,1)S(1)}, u32[]{:S(2)}, u32[]{:S(2)}) collective-permute-start(bf16[2,4,64,128]{3,2,1,0:T(8,128)(2,1)S(1)} %slice.129), channel_id=1, source_target_pairs={{0,8},{4,12},{8,0},{12,4},{16,24},{20,28},{24,16},{28,20},{1,9},{5... | collective-permute-start | bytes 393224 | tf_op jit(solution)/shard_map/ppermute | solution.py:44
  112.0 8.4 %collective-permute-start.16 = (bf16[2,4,32,256]{3,2,1,0:T(8,128)(2,1)S(1)}, bf16[2,4,32,256]{3,2,1,0:T(8,128)(2,1)S(1)}, u32[]{:S(2)}, u32[]{:S(2)}) collective-permute-start(bf16[2,4,32,256]{3,2,1,0:T(8,128)(2,1)S(1)} %slice.128), channel_id=1, source_target_pairs={{0,16},{4,20},{8,24},{12,28},{16,0},{20,4},{24,8},{28,12},{1,17},{... | collective-permute-start | bytes 393224 | tf_op jit(solution)/shard_map/ppermute | solution.py:44
  114.1 7.0 %collective-permute-start.18 = (bf16[2,4,32,128]{3,2,1,0:T(8,128)(2,1)S(1)}, bf16[2,4,32,128]{3,2,1,0:T(8,128)(2,1)S(1)}, u32[]{:S(2)}, u32[]{:S(2)}) collective-permute-start(bf16[2,4,32,128]{3,2,1,0:T(8,128)(2,1)S(1)} %slice.133), channel_id=1, source_target_pairs={{0,16},{4,20},{8,24},{12,28},{16,0},{20,4},{24,8},{28,12},{1,17},{... | collective-permute-start | bytes 196616 | tf_op jit(solution)/shard_map/ppermute | solution.py:44
  123.6 5.7 %collective-permute-start.21 = (f32[2,64,128]{2,1,0:T(8,128)S(1)}, f32[2,64,128]{2,1,0:T(8,128)S(1)}, u32[]{:S(2)}, u32[]{:S(2)}) collective-permute-start(f32[2,64,128]{2,1,0:T(8,128)S(1)} %get-tuple-element.79.refs_0_), channel_id=1, source_target_pairs={{0,3},{1,2},{2,1},{3,0},{4,7},{5,6},{6,5},{7,4},{8,11},{9,10},{10,... | collective-permute-start | bytes 196616 | tf_op jit(solution)/shard_map/ppermute | solution.py:44
  126.2 4.3 %collective-permute-start.20 = (f32[2,64,128]{2,1,0:T(8,128)S(1)}, f32[2,64,128]{2,1,0:T(8,128)S(1)}, u32[]{:S(2)}, u32[]{:S(2)}) collective-permute-start(f32[2,64,128]{2,1,0:T(8,128)S(1)} %get-tuple-element.79.refs_0_), channel_id=1, source_target_pairs={{0,2},{1,3},{2,0},{3,1},{4,6},{5,7},{6,4},{7,5},{8,10},{9,11},{10,... | collective-permute-start | bytes 196616 | tf_op jit(solution)/shard_map/ppermute | solution.py:44
  126.7 4.3 %collective-permute-start.19 = (f32[2,64,128]{2,1,0:T(8,128)S(1)}, f32[2,64,128]{2,1,0:T(8,128)S(1)}, u32[]{:S(2)}, u32[]{:S(2)}) collective-permute-start(f32[2,64,128]{2,1,0:T(8,128)S(1)} %get-tuple-element.79.refs_0_), channel_id=1, source_target_pairs={{0,1},{1,0},{2,3},{3,2},{4,5},{5,4},{6,7},{7,6},{8,9},{9,8},{10,11... | collective-permute-start | bytes 196616 | tf_op jit(solution)/shard_map/ppermute | solution.py:44

commit v3 on v2

--- a/solution.py
+++ b/solution.py
@@ -308,10 +308,11 @@
     def rotate(unit, at, total):
         cosine = phase[unit, 0, at, :]
         sine = phase[unit, 1, at, :]
-        ahead_c = step[0, at, 48 + 8 * unit : 49 + 8 * unit]
-        ahead_s = step[1, at, 48 + 8 * unit : 49 + 8 * unit]
-        phase[unit, 0, at, :] = cosine * ahead_c - sine * ahead_s
-        phase[unit, 1, at, :] = cosine * ahead_s + sine * ahead_c
+        if more or near.shape[0] > 1:
+            ahead_c = step[0, at, 48 + 8 * unit : 49 + 8 * unit]
+            ahead_s = step[1, at, 48 + 8 * unit : 49 + 8 * unit]
+            phase[unit, 0, at, :] = cosine * ahead_c - sine * ahead_s
+            phase[unit, 1, at, :] = cosine * ahead_s + sine * ahead_c
         real = total[:, :LANES]
         imag = total[:, LANES:]
         return cosine * real - sine * imag, sine * real + cosine * imag
@@ -553,8 +554,28 @@
         halves[part] = (total[:, :, :half], arrived, stage + 1)
         return send
 
+    def advance_together(parts):
+        stage = stages - 1
+        total = jnp.concatenate([halves[p][0] + halves[p][1].astype(F32) for p in parts], axis=3)
+        half = total.shape[2] // 2
+        send = total[:, :, half:].astype(BF16)
+        arrived = swap(send, "pulse", 1 << stage)
+        for p in parts:
+            halves[p] = None
+        halves[parts[-1]] = (total[:, :, :half], arrived, stages)
+        return send
+
     for part in range(calls):
-        done = [advance(p) for p in range(part - 1) if halves[p][2] < stages]
+        done = []
+        for p in range(part - 1):
+            if halves[p] is None or halves[p][2] == stages:
+                continue
+            if calls == 5 and stages == 3 and p == 0 and part == 3:
+                continue
+            if calls == 5 and stages == 3 and p == 0 and part == 4:
+                done.append(advance_together([0, 1]))
+            else:
+                done.append(advance(p))
         if done:
             phase, done = lax.optimization_barrier((phase, done))
         keep, send, phase, *ahead = partial_spectrum(
@@ -568,10 +589,10 @@
         halves[part] = (keep, swap(send, "pulse", 1), 1)
     for stage in range(1, stages):
         for part in range(calls):
-            if halves[part][2] == stage:
+            if halves[part] is not None and halves[part][2] == stage:
                 advance(part)
-    kept = [half[0] for half in halves]
-    received = [half[1] for half in halves]
+    kept = [half[0] for half in halves if half is not None]
+    received = [half[1] for half in halves if half is not None]
     spectrum, cov = spectrum_and_covariance(kept, received, angles ** (-0.5))
     covs = [cov]
     distance = 1

time: 133 us -> 144 us (1.083)
  waiting for transfers between devices: 23.6 us -> 37.5 us
  starting transfers between devices: 23.2 us -> 21 us
    ppermute x22 -> x21, waiting for transfers between devices: 23.6 us -> 37.5 us  [swap(): return lax.ppermute(block, axis, [(i, i ^ distance) for i in range(count)])]
    ppermute x22 -> x21, starting transfers between devices: 23.2 us -> 21 us  [swap(): return lax.ppermute(block, axis, [(i, i ^ distance) for i in range(count)])]
  transfers between devices with their start and end apart: 22 -> 21, of which waited for: 8 -> 10; matrix products, arithmetic and copies ran while one was open for 1% -> 1% of each run, Pallas kernels for 37% -> 19%
where the time goes in v3:
time: 144 us
  Pallas kernels  81.7 us (57%)
  waiting for transfers between devices  37.5 us (26%)
  starting transfers between devices  21 us (15%)
  local copies, waits for them, and re-layouts  2.62 us (2%)
    pallas_call x5, Pallas kernels, partial_spectrum(): pl.pallas_call(functools.partial(main_kernel, start, classes, chunks > 0)...  54.7 us
    ppermute x21, waiting for transfers between devices, swap(): return lax.ppermute(block, axis, [(i, i ^ distance) for i in range(count)])  37.5 us
    ppermute x21, starting transfers between devices, swap(): return lax.ppermute(block, axis, [(i, i ^ distance) for i in range(count)])  21 us
    pallas_call x1, Pallas kernels, second_tables(): pl.pallas_call(functools.partial(second_kernel, ranges), in_specs=[SMEM]...  14.6 us
    pallas_call x1, Pallas kernels, first_tables(): pl.pallas_call(functools.partial(first_kernel, pulses), in_specs=[SMEM, V...  7.95 us
  transfers between devices with their start and end apart: 21, of which 10 were waited for; matrix products, arithmetic and copies ran while one was open for 1% of the time, Pallas kernels for 19%

profile of v3, /device:TPU:0, one launch (start us, length us, event | category | flops | bytes accessed | tf_op | source)
XLA Modules:
  0.0 143.9 jit_solution(18298812927419954625)
XLA Ops:
  0.5 0.9 copy-done.1
  1.4 0.8 copy-done.2
  2.2 0.7 copy-done.3
  3.0 3.6 %collective-permute-start.1 = (f32[16,1024]{1,0:T(8,128)S(1)}, f32[16,1024]{1,0:T(8,128)S(1)}, u32[]{:S(2)}, u32[]{:S(2)}) collective-permute-start(f32[16,1024]{1,0:T(8,128)S(1)} %get-tuple-element.45), channel_id=1, source_target_pairs={{0,16},{4,20},{8,24},{12,28},{16,0},{20,4},{24,8},{28,12},{1,17},{... | collective-permute-start | bytes 196616 | tf_op jit(solution)/shard_map/ppermute | solution.py:44
  6.6 1.3 collective-permute-start.2
  8.3 7.9 %first.1 = (bf16[2,1024,1024]{2,1,0:T(8,128)(2,1)S(1)}, bf16[2048,1024]{1,0:T(8,128)(2,1)S(1)}) custom-call(s32[4]{0:T(128)S(1)} %pad_add_fusion.scalars, f32[40,1024]{1,0:T(8,128)S(1)} %get-tuple-element.43.mine), custom_call_target="tpu_custom_call" | custom-call | flops 4194304000 | bytes 8388608 | tf_op jit(solution)/shard_map/first/pallas_call | solution.py:158
  16.3 14.6 %second.1 = (bf16[2,1024,1024]{2,1,0:T(8,128)(2,1)S(1)}, bf16[4,1024,1024]{2,1,0:T(8,128)(2,1)S(1)}, f32[7,2,1024,128]{3,2,1,0:T(8,128)S(1)}, f32[2,1024,128]{2,...) custom-call(s32[4]{0:T(128)S(1)} %pad_add_fusion.scalars, ...), custom_call_target="tpu_custom_call" | custom-call | flops 8388608000 | bytes 12582912 | tf_op jit(solution)/shard_map/second/pallas_call | solution.py:243
  30.9 13.5 %main.5 = (f32[2,4,128,256]{3,2,1,0:T(8,128)S(1)}, bf16[2,4,128,256]{3,2,1,0:T(8,128)(2,1)S(1)}, f32[7,2,1024,128]{3,2,1,0:T(8,128)S(1)}, bf16[2,1024,256]{2,1,0:T(8,128)(2,1)S(1)}, bf16[2,1024,256]{2,1,0:T(8,128)(2,1)S(1)}) custom-call(bf16[2,1024,256]{2,1,0:T(8,128)(2,1)S(1)} %get-tuple-element.46.near, ...), custom_call_target="tpu_custom_call", output_to_operand_aliasing={{2}: (7, {})} | custom-call | flops 10737418240 | bytes 1048576 | tf_op jit(solution)/shard_map/main/pallas_call | solution.py:375
  44.5 13.7 %main.6 = (f32[2,4,128,256]{3,2,1,0:T(8,128)S(1)}, bf16[2,4,128,256]{3,2,1,0:T(8,128)(2,1)S(1)}, f32[7,2,1024,128]{3,2,1,0:T(8,128)S(1)}, bf16[2,1024,256]{2,1,0:T(8,128)(2,1)S(1)}, bf16[2,1024,256]{2,1,0:T(8,128)(2,1)S(1)}) custom-call(bf16[2,1024,256]{2,1,0:T(8,128)(2,1)S(1)} %get-tuple-element.56.near, ...), custom_call_target="tpu_custom_call", output_to_operand_aliasing={{2}: (7, {})} | custom-call | flops 10737418240 | bytes 1048576 | tf_op jit(solution)/shard_map/main/pallas_call | solution.py:375
  58.9 1.4 collective-permute-done.6
  60.4 13.6 %main.7 = (f32[2,4,128,256]{3,2,1,0:T(8,128)S(1)}, bf16[2,4,128,256]{3,2,1,0:T(8,128)(2,1)S(1)}, f32[7,2,1024,128]{3,2,1,0:T(8,128)S(1)}, bf16[1,1024,256]{2,1,0:T(8,128)(2,1)S(1)}, bf16[1,1024,256]{2,1,0:T(8,128)(2,1)S(1)}) custom-call(bf16[2,1024,256]{2,1,0:T(8,128)(2,1)S(1)} %get-tuple-element.61.near, ...), custom_call_target="tpu_custom_call", output_to_operand_aliasing={{2}: (7, {})} | custom-call | flops 10737418240 | bytes 1048576 | tf_op jit(solution)/shard_map/main/pallas_call | solution.py:375
  74.0 7.6 %main.8 = (f32[2,4,128,128]{3,2,1,0:T(8,128)S(1)}, bf16[2,4,128,128]{3,2,1,0:T(8,128)(2,1)S(1)}, f32[7,2,1024,128]{3,2,1,0:T(8,128)S(1)}, bf16[1,1024,256]{2,1,0:T(8,128)(2,1)S(1)}, bf16[1,1024,256]{2,1,0:T(8,128)(2,1)S(1)}) custom-call(bf16[1,1024,256]{2,1,0:T(8,128)(2,1)S(1)} %get-tuple-element.67.near, ...), custom_call_target="tpu_custom_call", output_to_operand_aliasing={{2}: (7, {})} | custom-call | flops 5368709120 | bytes 1048576 | tf_op jit(solution)/shard_map/main/pallas_call | solution.py:375
  82.1 1.8 %collective-permute-start.5 = (bf16[2,4,64,256]{3,2,1,0:T(8,128)(2,1)S(1)}, bf16[2,4,64,256]{3,2,1,0:T(8,128)(2,1)S(1)}, u32[]{:S(2)}, u32[]{:S(2)}) collective-permute-start(bf16[2,4,64,256]{3,2,1,0:T(8,128)(2,1)S(1)} %slice.120), channel_id=1, source_target_pairs={{0,8},{4,12},{8,0},{12,4},{16,24},{20,28},{24,16},{28,20},{1,9},{5... | collective-permute-start | bytes 786440 | tf_op jit(solution)/shard_map/ppermute | solution.py:44
  84.2 1.9 %collective-permute-start.11 = (bf16[2,4,64,128]{3,2,1,0:T(8,128)(2,1)S(1)}, bf16[2,4,64,128]{3,2,1,0:T(8,128)(2,1)S(1)}, u32[]{:S(2)}, u32[]{:S(2)}) collective-permute-start(bf16[2,4,64,128]{3,2,1,0:T(8,128)(2,1)S(1)} %slice.123), channel_id=1, source_target_pairs={{0,8},{4,12},{8,0},{12,4},{16,24},{20,28},{24,16},{28,20},{1,9},{5... | collective-permute-start | bytes 393224 | tf_op jit(solution)/shard_map/ppermute | solution.py:44
  86.1 5.2 %collective-permute-done.5 = bf16[2,4,64,256]{3,2,1,0:T(8,128)(2,1)S(1)} collective-permute-done((bf16[2,4,64,256]{3,2,1,0:T(8,128)(2,1)S(1)}, bf16[2,4,64,256]{3,2,1,0:T(8,128)(2,1)S(1)}, u32[]{:S(2)}, u32[]{:S(2)}) %collective-permute-start.5) | collective-permute-done | bytes 262176 | tf_op jit(solution)/shard_map/ppermute | solution.py:44
  91.3 5.6 %collective-permute-done.7 = bf16[2,4,64,256]{3,2,1,0:T(8,128)(2,1)S(1)} collective-permute-done((bf16[2,4,64,256]{3,2,1,0:T(8,128)(2,1)S(1)}, bf16[2,4,64,256]{3,2,1,0:T(8,128)(2,1)S(1)}, u32[]{:S(2)}, u32[]{:S(2)}) %collective-permute-start.7) | collective-permute-done | bytes 262176 | tf_op jit(solution)/shard_map/ppermute | solution.py:44
  97.2 6.3 %main.9 = (f32[2,4,128,128]{3,2,1,0:T(8,128)S(1)}, bf16[2,4,128,128]{3,2,1,0:T(8,128)(2,1)S(1)}, f32[7,2,1024,128]{3,2,1,0:T(8,128)S(1)}) custom-call(bf16[1,1024,256]{2,1,0:T(8,128)(2,1)S(1)} %get-tuple-element.73.near, bf16[1,1024,256]{2,1,0:T(8,128)(2,1)S(1)} %get-tuple-element.74.far, ...), custom_call_target="tpu_custom_call", output_to_operand_aliasing={{2}: (7, {})} | custom-call | flops 5368709120 | bytes 1048576 | tf_op jit(solution)/shard_map/main/pallas_call | solution.py:375
  103.5 2.9 %collective-permute-start.14 = (bf16[2,4,32,512]{3,2,1,0:T(8,128)(2,1)S(1)}, bf16[2,4,32,512]{3,2,1,0:T(8,128)(2,1)S(1)}, u32[]{:S(2)}, u32[]{:S(2)}) collective-permute-start(bf16[2,4,32,512]{3,2,1,0:T(8,128)(2,1)S(1)} %fusion.1), channel_id=1, source_target_pairs={{0,16},{4,20},{8,24},{12,28},{16,0},{20,4},{24,8},{28,12},{1,17},{... | collective-permute-start | bytes 786440 | tf_op jit(solution)/shard_map/ppermute | solution.py:44
  106.4 0.7 collective-permute-start.9
  107.1 1.3 collective-permute-start.16
  108.8 12.5 %collective-permute-done.9 = bf16[2,4,64,256]{3,2,1,0:T(8,128)(2,1)S(1)} collective-permute-done((bf16[2,4,64,256]{3,2,1,0:T(8,128)(2,1)S(1)}, bf16[2,4,64,256]{3,2,1,0:T(8,128)(2,1)S(1)}, u32[]{:S(2)}, u32[]{:S(2)}) %collective-permute-start.9) | collective-permute-done | bytes 262176 | tf_op jit(solution)/shard_map/ppermute | solution.py:44
  121.5 3.4 %collective-permute-done.13 = bf16[2,4,64,128]{3,2,1,0:T(8,128)(2,1)S(1)} collective-permute-done((bf16[2,4,64,128]{3,2,1,0:T(8,128)(2,1)S(1)}, bf16[2,4,64,128]{3,2,1,0:T(8,128)(2,1)S(1)}, u32[]{:S(2)}, u32[]{:S(2)}) %collective-permute-start.13) | collective-permute-done | bytes 131104 | tf_op jit(solution)/shard_map/ppermute | solution.py:44
  124.9 1.5 %collective-permute-start.17 = (bf16[2,4,32,128]{3,2,1,0:T(8,128)(2,1)S(1)}, bf16[2,4,32,128]{3,2,1,0:T(8,128)(2,1)S(1)}, u32[]{:S(2)}, u32[]{:S(2)}) collective-permute-start(bf16[2,4,32,128]{3,2,1,0:T(8,128)(2,1)S(1)} %slice.124), channel_id=1, source_target_pairs={{0,16},{4,20},{8,24},{12,28},{16,0},{20,4},{24,8},{28,12},{1,17},{... | collective-permute-start | bytes 196616 | tf_op jit(solution)/shard_map/ppermute | solution.py:44
  126.6 2.6 %collective-permute-done.15.refs_5_ = bf16[2,4,32,256]{3,2,1,0:T(8,128)(2,1)S(1)} collective-permute-done((bf16[2,4,32,256]{3,2,1,0:T(8,128)(2,1)S(1)}, bf16[2,4,32,256]{3,2,1,0:T(8,128)(2,1)S(1)}, u32[]{:S(2)}, u32[]{:S(2)}) %collective-permute-start.15) | collective-permute-done | bytes 131104 | tf_op jit(solution)/shard_map/ppermute | solution.py:44
  129.2 2.2 %collective-permute-done.17.refs_7_ = bf16[2,4,32,128]{3,2,1,0:T(8,128)(2,1)S(1)} collective-permute-done((bf16[2,4,32,128]{3,2,1,0:T(8,128)(2,1)S(1)}, bf16[2,4,32,128]{3,2,1,0:T(8,128)(2,1)S(1)}, u32[]{:S(2)}, u32[]{:S(2)}) %collective-permute-start.17) | collective-permute-done | bytes 65568 | tf_op jit(solution)/shard_map/ppermute | solution.py:44
  131.3 2.5 %covariance.1 = (f32[2,4,32,1024]{3,2,1,0:T(8,128)S(1)}, f32[2,64,128]{2,1,0:T(8,128)S(1)}) custom-call(f32[2,4,32,512]{3,2,1,0:T(8,128)S(1)} %fusion.refs_0_, f32[2,4,32,256]{3,2,1,0:T(8,128)S(1)} %slice.89.refs_1_, f32[2,4,32,128]{3,2,1,0:T(8,128)S(1)} %slice.92.refs_2_, f32[2,4,32,128]{3,2,1,0:T(8,128)S(1)} %slice.95.refs_3_, ...), custom_call_target="tpu_custom_call" | custom-call | tf_op jit(solution)/shard_map/covariance/pallas_call | solution.py:440
  133.8 1.6 %collective-permute-start.18 = (f32[2,64,128]{2,1,0:T(8,128)S(1)}, f32[2,64,128]{2,1,0:T(8,128)S(1)}, u32[]{:S(2)}, u32[]{:S(2)}) collective-permute-start(f32[2,64,128]{2,1,0:T(8,128)S(1)} %get-tuple-element.79.refs_0_), channel_id=1, source_target_pairs={{0,1},{1,0},{2,3},{3,2},{4,5},{5,4},{6,7},{7,6},{8,9},{9,8},{10,11... | collective-permute-start | bytes 196616 | tf_op jit(solution)/shard_map/ppermute | solution.py:44
  135.4 1.5 %collective-permute-start.19 = (f32[2,64,128]{2,1,0:T(8,128)S(1)}, f32[2,64,128]{2,1,0:T(8,128)S(1)}, u32[]{:S(2)}, u32[]{:S(2)}) collective-permute-start(f32[2,64,128]{2,1,0:T(8,128)S(1)} %get-tuple-element.79.refs_0_), channel_id=1, source_target_pairs={{0,2},{1,3},{2,0},{3,1},{4,6},{5,7},{6,4},{7,5},{8,10},{9,11},{10,... | collective-permute-start | bytes 196616 | tf_op jit(solution)/shard_map/ppermute | solution.py:44
  137.4 0.9 collective-permute-done.18.refs_1_
  138.3 1.4 collective-permute-done.19.refs_2_
  139.7 2.4 %collective-permute-done.20.refs_3_ = f32[2,64,128]{2,1,0:T(8,128)S(1)} collective-permute-done((f32[2,64,128]{2,1,0:T(8,128)S(1)}, f32[2,64,128]{2,1,0:T(8,128)S(1)}, u32[]{:S(2)}, u32[]{:S(2)}) %collective-permute-start.20) | collective-permute-done | bytes 65568 | tf_op jit(solution)/shard_map/ppermute | solution.py:44
  142.1 1.8 %focus.1 = f32[2,128,1024]{2,1,0:T(8,128)} custom-call(f32[2,64,128]{2,1,0:T(8,128)S(1)} %get-tuple-element.79.refs_0_, f32[2,64,128]{2,1,0:T(8,128)S(1)} %collective-permute-done.18.refs_1_, f32[2,64,128]{2,1,0:T(8,128)S(1)} %collective-permute-done.19.refs_2_, f32[2,64,128]{2,1,0:T(8,128)S(1)} %collective-permute-done.20.refs_3_, ...), custom_call_target="tpu_custom_call" | custom-call | tf_op jit(solution)/shard_map/focus/pallas_call | solution.py:504
  (52 shorter events, 4.1 us)
Async XLA Ops:
  0.0 16.2 %collective-permute-start.3 = (bf16[2,1024,1024]{2,1,0:T(8,128)(2,1)}, bf16[2,1024,1024]{2,1,0:T(8,128)(2,1)}, u32[]{:S(2)}, u32[]{:S(2)}) collective-permute-start(bf16[2,1024,1024]{2,1,0:T(8,128)(2,1)} %refs_0_.7), channel_id=1, source_target_pairs={{0,4},{4,0},{8,12},{12,8},{16,20},{20,16},{24,28},{28,24},{1,5},{5... | collective-permute-start | bytes 12582920 | tf_op jit(solution)/shard_map/ppermute | solution.py:44
  0.5 0.9 copy-start.1
  1.4 0.8 copy-start.2
  2.2 0.7 copy-start.3
  3.0 13.3 %collective-permute-start.1 = (f32[16,1024]{1,0:T(8,128)S(1)}, f32[16,1024]{1,0:T(8,128)S(1)}, u32[]{:S(2)}, u32[]{:S(2)}) collective-permute-start(f32[16,1024]{1,0:T(8,128)S(1)} %get-tuple-element.45), channel_id=1, source_target_pairs={{0,16},{4,20},{8,24},{12,28},{16,0},{20,4},{24,8},{28,12},{1,17},{... | collective-permute-start | bytes 196616 | tf_op jit(solution)/shard_map/ppermute | solution.py:44
  6.6 9.6 %collective-permute-start.2 = (f32[16,1024]{1,0:T(8,128)S(1)}, f32[16,1024]{1,0:T(8,128)S(1)}, u32[]{:S(2)}, u32[]{:S(2)}) collective-permute-start(f32[16,1024]{1,0:T(8,128)S(1)} %get-tuple-element.45), channel_id=1, source_target_pairs={{0,24},{4,28},{8,16},{12,20},{16,8},{20,12},{24,0},{28,4},{1,25},{... | collective-permute-start | bytes 196616 | tf_op jit(solution)/shard_map/ppermute | solution.py:44
  7.9 8.3 %collective-permute-start = (f32[24,1024]{1,0:T(8,128)S(1)}, f32[24,1024]{1,0:T(8,128)S(1)}, u32[]{:S(2)}, u32[]{:S(2)}) collective-permute-start(f32[24,1024]{1,0:T(8,128)S(1)} %get-tuple-element.44), channel_id=1, source_target_pairs={{0,8},{4,12},{8,0},{12,4},{16,24},{20,28},{24,16},{28,20},{1,9},{5... | collective-permute-start | bytes 294920 | tf_op jit(solution)/shard_map/ppermute | solution.py:44
  8.2 8.0 %copy-start = (bf16[2,1024,1024]{2,1,0:T(8,128)(2,1)S(1)}, bf16[2,1024,1024]{2,1,0:T(8,128)(2,1)}, u32[]{:S(2)}) copy-start(bf16[2,1024,1024]{2,1,0:T(8,128)(2,1)} %refs_0_.7) | copy-start | bytes 12582916
  44.4 14.3 %collective-permute-start.4 = (bf16[2,4,128,256]{3,2,1,0:T(8,128)(2,1)S(1)}, bf16[2,4,128,256]{3,2,1,0:T(8,128)(2,1)S(1)}, u32[]{:S(2)}, u32[]{:S(2)}) collective-permute-start(bf16[2,4,128,256]{3,2,1,0:T(8,128)(2,1)S(1)} %get-tuple-element.55), channel_id=1, source_target_pairs={{0,4},{4,0},{8,12},{12,8},{16,20},{20,16},{24,28},{28,24},{1,5},{5... | collective-permute-start | bytes 1572872 | tf_op jit(solution)/shard_map/ppermute | solution.py:44
  58.2 2.1 %collective-permute-start.6 = (bf16[2,4,128,256]{3,2,1,0:T(8,128)(2,1)S(1)}, bf16[2,4,128,256]{3,2,1,0:T(8,128)(2,1)S(1)}, u32[]{:S(2)}, u32[]{:S(2)}) collective-permute-start(bf16[2,4,128,256]{3,2,1,0:T(8,128)(2,1)S(1)} %get-tuple-element.60), channel_id=1, source_target_pairs={{0,4},{4,0},{8,12},{12,8},{16,20},{20,16},{24,28},{28,24},{1,5},{5... | collective-permute-start | bytes 1572872 | tf_op jit(solution)/shard_map/ppermute | solution.py:44
  81.7 2.5 %collective-permute-start.10 = (bf16[2,4,128,128]{3,2,1,0:T(8,128)(2,1)S(1)}, bf16[2,4,128,128]{3,2,1,0:T(8,128)(2,1)S(1)}, u32[]{:S(2)}, u32[]{:S(2)}) collective-permute-start(bf16[2,4,128,128]{3,2,1,0:T(8,128)(2,1)S(1)} %get-tuple-element.72), channel_id=1, source_target_pairs={{0,4},{4,0},{8,12},{12,8},{16,20},{20,16},{24,28},{28,24},{1,5},{5... | collective-permute-start | bytes 786440 | tf_op jit(solution)/shard_map/ppermute | solution.py:44
  82.1 9.2 %collective-permute-start.5 = (bf16[2,4,64,256]{3,2,1,0:T(8,128)(2,1)S(1)}, bf16[2,4,64,256]{3,2,1,0:T(8,128)(2,1)S(1)}, u32[]{:S(2)}, u32[]{:S(2)}) collective-permute-start(bf16[2,4,64,256]{3,2,1,0:T(8,128)(2,1)S(1)} %slice.120), channel_id=1, source_target_pairs={{0,8},{4,12},{8,0},{12,4},{16,24},{20,28},{24,16},{28,20},{1,9},{5... | collective-permute-start | bytes 786440 | tf_op jit(solution)/shard_map/ppermute | solution.py:44
  83.9 13.0 %collective-permute-start.7 = (bf16[2,4,64,256]{3,2,1,0:T(8,128)(2,1)S(1)}, bf16[2,4,64,256]{3,2,1,0:T(8,128)(2,1)S(1)}, u32[]{:S(2)}, u32[]{:S(2)}) collective-permute-start(bf16[2,4,64,256]{3,2,1,0:T(8,128)(2,1)S(1)} %slice.119), channel_id=1, source_target_pairs={{0,8},{4,12},{8,0},{12,4},{16,24},{20,28},{24,16},{28,20},{1,9},{5... | collective-permute-start | bytes 786440 | tf_op jit(solution)/shard_map/ppermute | solution.py:44
  84.1 12.9 %collective-permute-start.8 = (bf16[2,4,128,256]{3,2,1,0:T(8,128)(2,1)S(1)}, bf16[2,4,128,256]{3,2,1,0:T(8,128)(2,1)S(1)}, u32[]{:S(2)}, u32[]{:S(2)}) collective-permute-start(bf16[2,4,128,256]{3,2,1,0:T(8,128)(2,1)S(1)} %get-tuple-element.66), channel_id=1, source_target_pairs={{0,4},{4,0},{8,12},{12,8},{16,20},{20,16},{24,28},{28,24},{1,5},{5... | collective-permute-start | bytes 1572872 | tf_op jit(solution)/shard_map/ppermute | solution.py:44
  84.2 22.9 %collective-permute-start.11 = (bf16[2,4,64,128]{3,2,1,0:T(8,128)(2,1)S(1)}, bf16[2,4,64,128]{3,2,1,0:T(8,128)(2,1)S(1)}, u32[]{:S(2)}, u32[]{:S(2)}) collective-permute-start(bf16[2,4,64,128]{3,2,1,0:T(8,128)(2,1)S(1)} %slice.123), channel_id=1, source_target_pairs={{0,8},{4,12},{8,0},{12,4},{16,24},{20,28},{24,16},{28,20},{1,9},{5... | collective-permute-start | bytes 393224 | tf_op jit(solution)/shard_map/ppermute | solution.py:44
  103.5 5.0 %collective-permute-start.12 = (bf16[2,4,128,128]{3,2,1,0:T(8,128)(2,1)S(1)}, bf16[2,4,128,128]{3,2,1,0:T(8,128)(2,1)S(1)}, u32[]{:S(2)}, u32[]{:S(2)}) collective-permute-start(bf16[2,4,128,128]{3,2,1,0:T(8,128)(2,1)S(1)} %get-tuple-element.78), channel_id=1, source_target_pairs={{0,4},{4,0},{8,12},{12,8},{16,20},{20,16},{24,28},{28,24},{1,5},{5... | collective-permute-start | bytes 786440 | tf_op jit(solution)/shard_map/ppermute | solution.py:44
  103.5 23.0 %collective-permute-start.14 = (bf16[2,4,32,512]{3,2,1,0:T(8,128)(2,1)S(1)}, bf16[2,4,32,512]{3,2,1,0:T(8,128)(2,1)S(1)}, u32[]{:S(2)}, u32[]{:S(2)}) collective-permute-start(bf16[2,4,32,512]{3,2,1,0:T(8,128)(2,1)S(1)} %fusion.1), channel_id=1, source_target_pairs={{0,16},{4,20},{8,24},{12,28},{16,0},{20,4},{24,8},{28,12},{1,17},{... | collective-permute-start | bytes 786440 | tf_op jit(solution)/shard_map/ppermute | solution.py:44
  106.4 14.9 %collective-permute-start.9 = (bf16[2,4,64,256]{3,2,1,0:T(8,128)(2,1)S(1)}, bf16[2,4,64,256]{3,2,1,0:T(8,128)(2,1)S(1)}, u32[]{:S(2)}, u32[]{:S(2)}) collective-permute-start(bf16[2,4,64,256]{3,2,1,0:T(8,128)(2,1)S(1)} %slice.118), channel_id=1, source_target_pairs={{0,8},{4,12},{8,0},{12,4},{16,24},{20,28},{24,16},{28,20},{1,9},{5... | collective-permute-start | bytes 786440 | tf_op jit(solution)/shard_map/ppermute | solution.py:44
  107.1 19.4 %collective-permute-start.16 = (bf16[2,4,32,128]{3,2,1,0:T(8,128)(2,1)S(1)}, bf16[2,4,32,128]{3,2,1,0:T(8,128)(2,1)S(1)}, u32[]{:S(2)}, u32[]{:S(2)}) collective-permute-start(bf16[2,4,32,128]{3,2,1,0:T(8,128)(2,1)S(1)} %slice.125), channel_id=1, source_target_pairs={{0,16},{4,20},{8,24},{12,28},{16,0},{20,4},{24,8},{28,12},{1,17},{... | collective-permute-start | bytes 196616 | tf_op jit(solution)/shard_map/ppermute | solution.py:44
  108.5 16.3 %collective-permute-start.13 = (bf16[2,4,64,128]{3,2,1,0:T(8,128)(2,1)S(1)}, bf16[2,4,64,128]{3,2,1,0:T(8,128)(2,1)S(1)}, u32[]{:S(2)}, u32[]{:S(2)}) collective-permute-start(bf16[2,4,64,128]{3,2,1,0:T(8,128)(2,1)S(1)} %slice.122), channel_id=1, source_target_pairs={{0,8},{4,12},{8,0},{12,4},{16,24},{20,28},{24,16},{28,20},{1,9},{5... | collective-permute-start | bytes 393224 | tf_op jit(solution)/shard_map/ppermute | solution.py:44
  121.4 7.7 %collective-permute-start.15 = (bf16[2,4,32,256]{3,2,1,0:T(8,128)(2,1)S(1)}, bf16[2,4,32,256]{3,2,1,0:T(8,128)(2,1)S(1)}, u32[]{:S(2)}, u32[]{:S(2)}) collective-permute-start(bf16[2,4,32,256]{3,2,1,0:T(8,128)(2,1)S(1)} %slice.121), channel_id=1, source_target_pairs={{0,16},{4,20},{8,24},{12,28},{16,0},{20,4},{24,8},{28,12},{1,17},{... | collective-permute-start | bytes 393224 | tf_op jit(solution)/shard_map/ppermute | solution.py:44
  124.9 6.4 %collective-permute-start.17 = (bf16[2,4,32,128]{3,2,1,0:T(8,128)(2,1)S(1)}, bf16[2,4,32,128]{3,2,1,0:T(8,128)(2,1)S(1)}, u32[]{:S(2)}, u32[]{:S(2)}) collective-permute-start(bf16[2,4,32,128]{3,2,1,0:T(8,128)(2,1)S(1)} %slice.124), channel_id=1, source_target_pairs={{0,16},{4,20},{8,24},{12,28},{16,0},{20,4},{24,8},{28,12},{1,17},{... | collective-permute-start | bytes 196616 | tf_op jit(solution)/shard_map/ppermute | solution.py:44
  133.8 4.4 %collective-permute-start.18 = (f32[2,64,128]{2,1,0:T(8,128)S(1)}, f32[2,64,128]{2,1,0:T(8,128)S(1)}, u32[]{:S(2)}, u32[]{:S(2)}) collective-permute-start(f32[2,64,128]{2,1,0:T(8,128)S(1)} %get-tuple-element.79.refs_0_), channel_id=1, source_target_pairs={{0,1},{1,0},{2,3},{3,2},{4,5},{5,4},{6,7},{7,6},{8,9},{9,8},{10,11... | collective-permute-start | bytes 196616 | tf_op jit(solution)/shard_map/ppermute | solution.py:44
  135.4 4.3 %collective-permute-start.19 = (f32[2,64,128]{2,1,0:T(8,128)S(1)}, f32[2,64,128]{2,1,0:T(8,128)S(1)}, u32[]{:S(2)}, u32[]{:S(2)}) collective-permute-start(f32[2,64,128]{2,1,0:T(8,128)S(1)} %get-tuple-element.79.refs_0_), channel_id=1, source_target_pairs={{0,2},{1,3},{2,0},{3,1},{4,6},{5,7},{6,4},{7,5},{8,10},{9,11},{10,... | collective-permute-start | bytes 196616 | tf_op jit(solution)/shard_map/ppermute | solution.py:44
  136.9 5.2 %collective-permute-start.20 = (f32[2,64,128]{2,1,0:T(8,128)S(1)}, f32[2,64,128]{2,1,0:T(8,128)S(1)}, u32[]{:S(2)}, u32[]{:S(2)}) collective-permute-start(f32[2,64,128]{2,1,0:T(8,128)S(1)} %get-tuple-element.79.refs_0_), channel_id=1, source_target_pairs={{0,3},{1,2},{2,1},{3,0},{4,7},{5,6},{6,5},{7,4},{8,11},{9,10},{10,... | collective-permute-start | bytes 196616 | tf_op jit(solution)/shard_map/ppermute | solution.py:44

commit v4 on v2

--- a/solution.py
+++ b/solution.py
@@ -150,7 +150,7 @@
             )
         return 0
 
-    lax.fori_loop(0, BINS // 16, part, 0, unroll=2)
+    lax.fori_loop(0, BINS // 16, part, 0, unroll=4)
 
 
 def first_tables(scalars, mine, pulses):
@@ -233,7 +233,7 @@
         step[1, at, :] = sine
         return 0
 
-    lax.fori_loop(0, beams // 16, part, 0, unroll=2)
+    lax.fori_loop(0, beams // 16, part, 0, unroll=4)
     for copy in copies:
         copy.wait()
 
@@ -308,10 +308,11 @@
     def rotate(unit, at, total):
         cosine = phase[unit, 0, at, :]
         sine = phase[unit, 1, at, :]
-        ahead_c = step[0, at, 48 + 8 * unit : 49 + 8 * unit]
-        ahead_s = step[1, at, 48 + 8 * unit : 49 + 8 * unit]
-        phase[unit, 0, at, :] = cosine * ahead_c - sine * ahead_s
-        phase[unit, 1, at, :] = cosine * ahead_s + sine * ahead_c
+        if more or near.shape[0] > 1:
+            ahead_c = step[0, at, 48 + 8 * unit : 49 + 8 * unit]
+            ahead_s = step[1, at, 48 + 8 * unit : 49 + 8 * unit]
+            phase[unit, 0, at, :] = cosine * ahead_c - sine * ahead_s
+            phase[unit, 1, at, :] = cosine * ahead_s + sine * ahead_c
         real = total[:, :LANES]
         imag = total[:, LANES:]
         return cosine * real - sine * imag, sine * real + cosine * imag

time: 133 us -> 131 us (0.985)
  Pallas kernels: 82.2 us -> 80.2 us
where the time goes in v4:
time: 131 us
  Pallas kernels  80.2 us (61%)
  waiting for transfers between devices  23.6 us (18%)
  starting transfers between devices  23.2 us (18%)
  local copies, waits for them, and re-layouts  2.69 us (2%)
    pallas_call x5, Pallas kernels, partial_spectrum(): pl.pallas_call(functools.partial(main_kernel, start, classes, chunks > 0)...  54.7 us
    ppermute x22, waiting for transfers between devices, swap(): return lax.ppermute(block, axis, [(i, i ^ distance) for i in range(count)])  23.6 us
    ppermute x22, starting transfers between devices, swap(): return lax.ppermute(block, axis, [(i, i ^ distance) for i in range(count)])  23.2 us
    pallas_call x1, Pallas kernels, second_tables(): pl.pallas_call(functools.partial(second_kernel, ranges), in_specs=[SMEM]...  13.4 us
    pallas_call x1, Pallas kernels, first_tables(): pl.pallas_call(functools.partial(first_kernel, pulses), in_specs=[SMEM, V...  7.75 us
  transfers between devices with their start and end apart: 22, of which 8 were waited for; matrix products, arithmetic and copies ran while one was open for 1% of the time, Pallas kernels for 37%

profile of v4, /device:TPU:0, one launch (start us, length us, event | category | flops | bytes accessed | tf_op | source)
XLA Modules:
  0.0 130.8 jit_solution(10739719808254959681)
XLA Ops:
  0.5 0.9 copy-done.1
  1.4 0.8 copy-done.2
  2.2 0.7 copy-done.3
  3.0 4.7 %collective-permute-start.2 = (f32[16,1024]{1,0:T(8,128)S(1)}, f32[16,1024]{1,0:T(8,128)S(1)}, u32[]{:S(2)}, u32[]{:S(2)}) collective-permute-start(f32[16,1024]{1,0:T(8,128)S(1)} %get-tuple-element.45), channel_id=1, source_target_pairs={{0,24},{4,28},{8,16},{12,20},{16,8},{20,12},{24,0},{28,4},{1,25},{... | collective-permute-start | bytes 196616 | tf_op jit(solution)/shard_map/ppermute | solution.py:44
  7.6 0.6 collective-permute-start
  8.3 7.8 %first.1 = (bf16[2,1024,1024]{2,1,0:T(8,128)(2,1)S(1)}, bf16[2048,1024]{1,0:T(8,128)(2,1)S(1)}) custom-call(s32[4]{0:T(128)S(1)} %pad_add_fusion.scalars, f32[40,1024]{1,0:T(8,128)S(1)} %get-tuple-element.43.mine), custom_call_target="tpu_custom_call" | custom-call | flops 4194304000 | bytes 8388608 | tf_op jit(solution)/shard_map/first/pallas_call | solution.py:158
  16.1 13.4 %second.1 = (bf16[2,1024,1024]{2,1,0:T(8,128)(2,1)S(1)}, bf16[4,1024,1024]{2,1,0:T(8,128)(2,1)S(1)}, f32[7,2,1024,128]{3,2,1,0:T(8,128)S(1)}, f32[2,1024,128]{2,...) custom-call(s32[4]{0:T(128)S(1)} %pad_add_fusion.scalars, ...), custom_call_target="tpu_custom_call" | custom-call | flops 8388608000 | bytes 12582912 | tf_op jit(solution)/shard_map/second/pallas_call | solution.py:243
  29.5 13.5 %main.5 = (f32[2,4,128,256]{3,2,1,0:T(8,128)S(1)}, bf16[2,4,128,256]{3,2,1,0:T(8,128)(2,1)S(1)}, f32[7,2,1024,128]{3,2,1,0:T(8,128)S(1)}, bf16[2,1024,256]{2,1,0:T(8,128)(2,1)S(1)}, bf16[2,1024,256]{2,1,0:T(8,128)(2,1)S(1)}) custom-call(bf16[2,1024,256]{2,1,0:T(8,128)(2,1)S(1)} %get-tuple-element.46.near, ...), custom_call_target="tpu_custom_call", output_to_operand_aliasing={{2}: (7, {})} | custom-call | flops 10737418240 | bytes 1048576 | tf_op jit(solution)/shard_map/main/pallas_call | solution.py:375
  43.1 13.7 %main.6 = (f32[2,4,128,256]{3,2,1,0:T(8,128)S(1)}, bf16[2,4,128,256]{3,2,1,0:T(8,128)(2,1)S(1)}, f32[7,2,1024,128]{3,2,1,0:T(8,128)S(1)}, bf16[2,1024,256]{2,1,0:T(8,128)(2,1)S(1)}, bf16[2,1024,256]{2,1,0:T(8,128)(2,1)S(1)}) custom-call(bf16[2,1024,256]{2,1,0:T(8,128)(2,1)S(1)} %get-tuple-element.56.near, ...), custom_call_target="tpu_custom_call", output_to_operand_aliasing={{2}: (7, {})} | custom-call | flops 10737418240 | bytes 1048576 | tf_op jit(solution)/shard_map/main/pallas_call | solution.py:375
  56.8 0.6 collective-permute-start.6
  57.6 1.5 %collective-permute-start.5 = (bf16[2,4,64,256]{3,2,1,0:T(8,128)(2,1)S(1)}, bf16[2,4,64,256]{3,2,1,0:T(8,128)(2,1)S(1)}, u32[]{:S(2)}, u32[]{:S(2)}) collective-permute-start(bf16[2,4,64,256]{3,2,1,0:T(8,128)(2,1)S(1)} %slice.127), channel_id=1, source_target_pairs={{0,8},{4,12},{8,0},{12,4},{16,24},{20,28},{24,16},{28,20},{1,9},{5... | collective-permute-start | bytes 786440 | tf_op jit(solution)/shard_map/ppermute | solution.py:44
  59.0 13.5 %main.7 = (f32[2,4,128,256]{3,2,1,0:T(8,128)S(1)}, bf16[2,4,128,256]{3,2,1,0:T(8,128)(2,1)S(1)}, f32[7,2,1024,128]{3,2,1,0:T(8,128)S(1)}, bf16[1,1024,256]{2,1,0:T(8,128)(2,1)S(1)}, bf16[1,1024,256]{2,1,0:T(8,128)(2,1)S(1)}) custom-call(bf16[2,1024,256]{2,1,0:T(8,128)(2,1)S(1)} %get-tuple-element.61.near, ...), custom_call_target="tpu_custom_call", output_to_operand_aliasing={{2}: (7, {})} | custom-call | flops 10737418240 | bytes 1048576 | tf_op jit(solution)/shard_map/main/pallas_call | solution.py:375
  72.8 0.7 collective-permute-start.7
  73.6 7.6 %main.8 = (f32[2,4,128,128]{3,2,1,0:T(8,128)S(1)}, bf16[2,4,128,128]{3,2,1,0:T(8,128)(2,1)S(1)}, f32[7,2,1024,128]{3,2,1,0:T(8,128)S(1)}, bf16[1,1024,256]{2,1,0:T(8,128)(2,1)S(1)}, bf16[1,1024,256]{2,1,0:T(8,128)(2,1)S(1)}) custom-call(bf16[1,1024,256]{2,1,0:T(8,128)(2,1)S(1)} %get-tuple-element.67.near, ...), custom_call_target="tpu_custom_call", output_to_operand_aliasing={{2}: (7, {})} | custom-call | flops 5368709120 | bytes 1048576 | tf_op jit(solution)/shard_map/main/pallas_call | solution.py:375
  81.8 1.0 collective-permute-done.10
  82.9 1.5 %collective-permute-start.11 = (bf16[2,4,64,128]{3,2,1,0:T(8,128)(2,1)S(1)}, bf16[2,4,64,128]{3,2,1,0:T(8,128)(2,1)S(1)}, u32[]{:S(2)}, u32[]{:S(2)}) collective-permute-start(bf16[2,4,64,128]{3,2,1,0:T(8,128)(2,1)S(1)} %slice.131), channel_id=1, source_target_pairs={{0,8},{4,12},{8,0},{12,4},{16,24},{20,28},{24,16},{28,20},{1,9},{5... | collective-permute-start | bytes 393224 | tf_op jit(solution)/shard_map/ppermute | solution.py:44
  84.4 6.3 %main.9 = (f32[2,4,128,128]{3,2,1,0:T(8,128)S(1)}, bf16[2,4,128,128]{3,2,1,0:T(8,128)(2,1)S(1)}, f32[7,2,1024,128]{3,2,1,0:T(8,128)S(1)}) custom-call(bf16[1,1024,256]{2,1,0:T(8,128)(2,1)S(1)} %get-tuple-element.73.near, bf16[1,1024,256]{2,1,0:T(8,128)(2,1)S(1)} %get-tuple-element.74.far, ...), custom_call_target="tpu_custom_call", output_to_operand_aliasing={{2}: (7, {})} | custom-call | flops 5368709120 | bytes 1048576 | tf_op jit(solution)/shard_map/main/pallas_call | solution.py:375
  90.8 3.0 %collective-permute-start.14 = (bf16[2,4,32,256]{3,2,1,0:T(8,128)(2,1)S(1)}, bf16[2,4,32,256]{3,2,1,0:T(8,128)(2,1)S(1)}, u32[]{:S(2)}, u32[]{:S(2)}) collective-permute-start(bf16[2,4,32,256]{3,2,1,0:T(8,128)(2,1)S(1)} %slice.132), channel_id=1, source_target_pairs={{0,16},{4,20},{8,24},{12,28},{16,0},{20,4},{24,8},{28,12},{1,17},{... | collective-permute-start | bytes 393224 | tf_op jit(solution)/shard_map/ppermute | solution.py:44
  93.8 0.6 collective-permute-start.9
  94.4 2.5 %collective-permute-start.17 = (bf16[2,4,32,128]{3,2,1,0:T(8,128)(2,1)S(1)}, bf16[2,4,32,128]{3,2,1,0:T(8,128)(2,1)S(1)}, u32[]{:S(2)}, u32[]{:S(2)}) collective-permute-start(bf16[2,4,32,128]{3,2,1,0:T(8,128)(2,1)S(1)} %slice.134), channel_id=1, source_target_pairs={{0,16},{4,20},{8,24},{12,28},{16,0},{20,4},{24,8},{28,12},{1,17},{... | collective-permute-start | bytes 196616 | tf_op jit(solution)/shard_map/ppermute | solution.py:44
  97.0 1.9 %collective-permute-start.13 = (bf16[2,4,64,128]{3,2,1,0:T(8,128)(2,1)S(1)}, bf16[2,4,64,128]{3,2,1,0:T(8,128)(2,1)S(1)}, u32[]{:S(2)}, u32[]{:S(2)}) collective-permute-start(bf16[2,4,64,128]{3,2,1,0:T(8,128)(2,1)S(1)} %slice.129), channel_id=1, source_target_pairs={{0,8},{4,12},{8,0},{12,4},{16,24},{20,28},{24,16},{28,20},{1,9},{5... | collective-permute-start | bytes 393224 | tf_op jit(solution)/shard_map/ppermute | solution.py:44
  99.0 11.0 %collective-permute-done.9 = bf16[2,4,64,256]{3,2,1,0:T(8,128)(2,1)S(1)} collective-permute-done((bf16[2,4,64,256]{3,2,1,0:T(8,128)(2,1)S(1)}, bf16[2,4,64,256]{3,2,1,0:T(8,128)(2,1)S(1)}, u32[]{:S(2)}, u32[]{:S(2)}) %collective-permute-start.9) | collective-permute-done | bytes 262176 | tf_op jit(solution)/shard_map/ppermute | solution.py:44
  110.1 1.9 %collective-permute-done.13 = bf16[2,4,64,128]{3,2,1,0:T(8,128)(2,1)S(1)} collective-permute-done((bf16[2,4,64,128]{3,2,1,0:T(8,128)(2,1)S(1)}, bf16[2,4,64,128]{3,2,1,0:T(8,128)(2,1)S(1)}, u32[]{:S(2)}, u32[]{:S(2)}) %collective-permute-start.13) | collective-permute-done | bytes 131104 | tf_op jit(solution)/shard_map/ppermute | solution.py:44
  112.1 1.0 collective-permute-start.18
  113.3 5.2 %collective-permute-done.16.refs_7_ = bf16[2,4,32,256]{3,2,1,0:T(8,128)(2,1)S(1)} collective-permute-done((bf16[2,4,32,256]{3,2,1,0:T(8,128)(2,1)S(1)}, bf16[2,4,32,256]{3,2,1,0:T(8,128)(2,1)S(1)}, u32[]{:S(2)}, u32[]{:S(2)}) %collective-permute-start.16) | collective-permute-done | bytes 131104 | tf_op jit(solution)/shard_map/ppermute | solution.py:44
  118.4 0.7 collective-permute-done.18.refs_9_
  119.1 2.5 %covariance.1 = (f32[2,4,32,1024]{3,2,1,0:T(8,128)S(1)}, f32[2,64,128]{2,1,0:T(8,128)S(1)}) custom-call(f32[2,4,32,256]{3,2,1,0:T(8,128)S(1)} %slice.92.refs_0_, f32[2,4,32,256]{3,2,1,0:T(8,128)S(1)} %slice.95.refs_1_, f32[2,4,32,256]{3,2,1,0:T(8,128)S(1)} %slice.98.refs_2_, f32[2,4,32,128]{3,2,1,0:T(8,128)S(1)} %slice.102.refs_3_, ...), custom_call_target="tpu_custom_call" | custom-call | tf_op jit(solution)/shard_map/covariance/pallas_call | solution.py:440
  121.6 2.5 %collective-permute-start.21 = (f32[2,64,128]{2,1,0:T(8,128)S(1)}, f32[2,64,128]{2,1,0:T(8,128)S(1)}, u32[]{:S(2)}, u32[]{:S(2)}) collective-permute-start(f32[2,64,128]{2,1,0:T(8,128)S(1)} %get-tuple-element.79.refs_0_), channel_id=1, source_target_pairs={{0,3},{1,2},{2,1},{3,0},{4,7},{5,6},{6,5},{7,4},{8,11},{9,10},{10,... | collective-permute-start | bytes 196616 | tf_op jit(solution)/shard_map/ppermute | solution.py:44
  124.7 0.5 collective-permute-start.19
  125.2 2.1 %collective-permute-done.21.refs_3_ = f32[2,64,128]{2,1,0:T(8,128)S(1)} collective-permute-done((f32[2,64,128]{2,1,0:T(8,128)S(1)}, f32[2,64,128]{2,1,0:T(8,128)S(1)}, u32[]{:S(2)}, u32[]{:S(2)}) %collective-permute-start.21) | collective-permute-done | bytes 65568 | tf_op jit(solution)/shard_map/ppermute | solution.py:44
  127.3 1.1 collective-permute-done.20.refs_2_
  128.9 1.8 %focus.1 = f32[2,128,1024]{2,1,0:T(8,128)} custom-call(f32[2,64,128]{2,1,0:T(8,128)S(1)} %get-tuple-element.79.refs_0_, f32[2,64,128]{2,1,0:T(8,128)S(1)} %collective-permute-done.19.refs_1_, f32[2,64,128]{2,1,0:T(8,128)S(1)} %collective-permute-done.20.refs_2_, f32[2,64,128]{2,1,0:T(8,128)S(1)} %collective-permute-done.21.refs_3_, ...), custom_call_target="tpu_custom_call" | custom-call | tf_op jit(solution)/shard_map/focus/pallas_call | solution.py:504
  (56 shorter events, 3.3 us)
Async XLA Ops:
  0.0 16.1 %collective-permute-start.3 = (bf16[2,1024,1024]{2,1,0:T(8,128)(2,1)}, bf16[2,1024,1024]{2,1,0:T(8,128)(2,1)}, u32[]{:S(2)}, u32[]{:S(2)}) collective-permute-start(bf16[2,1024,1024]{2,1,0:T(8,128)(2,1)} %refs_0_.7), channel_id=1, source_target_pairs={{0,4},{4,0},{8,12},{12,8},{16,20},{20,16},{24,28},{28,24},{1,5},{5... | collective-permute-start | bytes 12582920 | tf_op jit(solution)/shard_map/ppermute | solution.py:44
  0.5 0.9 copy-start.1
  1.4 0.8 copy-start.2
  2.2 0.7 copy-start.3
  3.0 13.1 %collective-permute-start.2 = (f32[16,1024]{1,0:T(8,128)S(1)}, f32[16,1024]{1,0:T(8,128)S(1)}, u32[]{:S(2)}, u32[]{:S(2)}) collective-permute-start(f32[16,1024]{1,0:T(8,128)S(1)} %get-tuple-element.45), channel_id=1, source_target_pairs={{0,24},{4,28},{8,16},{12,20},{16,8},{20,12},{24,0},{28,4},{1,25},{... | collective-permute-start | bytes 196616 | tf_op jit(solution)/shard_map/ppermute | solution.py:44
  7.6 8.5 %collective-permute-start.1 = (f32[16,1024]{1,0:T(8,128)S(1)}, f32[16,1024]{1,0:T(8,128)S(1)}, u32[]{:S(2)}, u32[]{:S(2)}) collective-permute-start(f32[16,1024]{1,0:T(8,128)S(1)} %get-tuple-element.45), channel_id=1, source_target_pairs={{0,16},{4,20},{8,24},{12,28},{16,0},{20,4},{24,8},{28,12},{1,17},{... | collective-permute-start | bytes 196616 | tf_op jit(solution)/shard_map/ppermute | solution.py:44
  7.6 8.5 %collective-permute-start = (f32[24,1024]{1,0:T(8,128)S(1)}, f32[24,1024]{1,0:T(8,128)S(1)}, u32[]{:S(2)}, u32[]{:S(2)}) collective-permute-start(f32[24,1024]{1,0:T(8,128)S(1)} %get-tuple-element.44), channel_id=1, source_target_pairs={{0,8},{4,12},{8,0},{12,4},{16,24},{20,28},{24,16},{28,20},{1,9},{5... | collective-permute-start | bytes 294920 | tf_op jit(solution)/shard_map/ppermute | solution.py:44
  8.3 7.8 %copy-start = (bf16[2,1024,1024]{2,1,0:T(8,128)(2,1)S(1)}, bf16[2,1024,1024]{2,1,0:T(8,128)(2,1)}, u32[]{:S(2)}) copy-start(bf16[2,1024,1024]{2,1,0:T(8,128)(2,1)} %refs_0_.7) | copy-start | bytes 12582916
  43.1 14.3 %collective-permute-start.4 = (bf16[2,4,128,256]{3,2,1,0:T(8,128)(2,1)S(1)}, bf16[2,4,128,256]{3,2,1,0:T(8,128)(2,1)S(1)}, u32[]{:S(2)}, u32[]{:S(2)}) collective-permute-start(bf16[2,4,128,256]{3,2,1,0:T(8,128)(2,1)S(1)} %get-tuple-element.55), channel_id=1, source_target_pairs={{0,4},{4,0},{8,12},{12,8},{16,20},{20,16},{24,28},{28,24},{1,5},{5... | collective-permute-start | bytes 1572872 | tf_op jit(solution)/shard_map/ppermute | solution.py:44
  56.8 15.8 %collective-permute-start.6 = (bf16[2,4,128,256]{3,2,1,0:T(8,128)(2,1)S(1)}, bf16[2,4,128,256]{3,2,1,0:T(8,128)(2,1)S(1)}, u32[]{:S(2)}, u32[]{:S(2)}) collective-permute-start(bf16[2,4,128,256]{3,2,1,0:T(8,128)(2,1)S(1)} %get-tuple-element.60), channel_id=1, source_target_pairs={{0,4},{4,0},{8,12},{12,8},{16,20},{20,16},{24,28},{28,24},{1,5},{5... | collective-permute-start | bytes 1572872 | tf_op jit(solution)/shard_map/ppermute | solution.py:44
  57.6 16.0 %collective-permute-start.5 = (bf16[2,4,64,256]{3,2,1,0:T(8,128)(2,1)S(1)}, bf16[2,4,64,256]{3,2,1,0:T(8,128)(2,1)S(1)}, u32[]{:S(2)}, u32[]{:S(2)}) collective-permute-start(bf16[2,4,64,256]{3,2,1,0:T(8,128)(2,1)S(1)} %slice.127), channel_id=1, source_target_pairs={{0,8},{4,12},{8,0},{12,4},{16,24},{20,28},{24,16},{28,20},{1,9},{5... | collective-permute-start | bytes 786440 | tf_op jit(solution)/shard_map/ppermute | solution.py:44
  72.6 9.1 %collective-permute-start.8 = (bf16[2,4,128,256]{3,2,1,0:T(8,128)(2,1)S(1)}, bf16[2,4,128,256]{3,2,1,0:T(8,128)(2,1)S(1)}, u32[]{:S(2)}, u32[]{:S(2)}) collective-permute-start(bf16[2,4,128,256]{3,2,1,0:T(8,128)(2,1)S(1)} %get-tuple-element.66), channel_id=1, source_target_pairs={{0,4},{4,0},{8,12},{12,8},{16,20},{20,16},{24,28},{28,24},{1,5},{5... | collective-permute-start | bytes 1572872 | tf_op jit(solution)/shard_map/ppermute | solution.py:44
  72.8 8.8 %collective-permute-start.7 = (bf16[2,4,64,256]{3,2,1,0:T(8,128)(2,1)S(1)}, bf16[2,4,64,256]{3,2,1,0:T(8,128)(2,1)S(1)}, u32[]{:S(2)}, u32[]{:S(2)}) collective-permute-start(bf16[2,4,64,256]{3,2,1,0:T(8,128)(2,1)S(1)} %slice.126), channel_id=1, source_target_pairs={{0,8},{4,12},{8,0},{12,4},{16,24},{20,28},{24,16},{28,20},{1,9},{5... | collective-permute-start | bytes 786440 | tf_op jit(solution)/shard_map/ppermute | solution.py:44
  81.2 1.6 %collective-permute-start.10 = (bf16[2,4,128,128]{3,2,1,0:T(8,128)(2,1)S(1)}, bf16[2,4,128,128]{3,2,1,0:T(8,128)(2,1)S(1)}, u32[]{:S(2)}, u32[]{:S(2)}) collective-permute-start(bf16[2,4,128,128]{3,2,1,0:T(8,128)(2,1)S(1)} %get-tuple-element.72), channel_id=1, source_target_pairs={{0,4},{4,0},{8,12},{12,8},{16,20},{20,16},{24,28},{28,24},{1,5},{5... | collective-permute-start | bytes 786440 | tf_op jit(solution)/shard_map/ppermute | solution.py:44
  82.9 11.5 %collective-permute-start.11 = (bf16[2,4,64,128]{3,2,1,0:T(8,128)(2,1)S(1)}, bf16[2,4,64,128]{3,2,1,0:T(8,128)(2,1)S(1)}, u32[]{:S(2)}, u32[]{:S(2)}) collective-permute-start(bf16[2,4,64,128]{3,2,1,0:T(8,128)(2,1)S(1)} %slice.131), channel_id=1, source_target_pairs={{0,8},{4,12},{8,0},{12,4},{16,24},{20,28},{24,16},{28,20},{1,9},{5... | collective-permute-start | bytes 393224 | tf_op jit(solution)/shard_map/ppermute | solution.py:44
  90.7 6.3 %collective-permute-start.12 = (bf16[2,4,128,128]{3,2,1,0:T(8,128)(2,1)S(1)}, bf16[2,4,128,128]{3,2,1,0:T(8,128)(2,1)S(1)}, u32[]{:S(2)}, u32[]{:S(2)}) collective-permute-start(bf16[2,4,128,128]{3,2,1,0:T(8,128)(2,1)S(1)} %get-tuple-element.78), channel_id=1, source_target_pairs={{0,4},{4,0},{8,12},{12,8},{16,20},{20,16},{24,28},{28,24},{1,5},{5... | collective-permute-start | bytes 786440 | tf_op jit(solution)/shard_map/ppermute | solution.py:44
  90.8 22.5 %collective-permute-start.14 = (bf16[2,4,32,256]{3,2,1,0:T(8,128)(2,1)S(1)}, bf16[2,4,32,256]{3,2,1,0:T(8,128)(2,1)S(1)}, u32[]{:S(2)}, u32[]{:S(2)}) collective-permute-start(bf16[2,4,32,256]{3,2,1,0:T(8,128)(2,1)S(1)} %slice.132), channel_id=1, source_target_pairs={{0,16},{4,20},{8,24},{12,28},{16,0},{20,4},{24,8},{28,12},{1,17},{... | collective-permute-start | bytes 393224 | tf_op jit(solution)/shard_map/ppermute | solution.py:44
  93.7 19.5 %collective-permute-start.15 = (bf16[2,4,32,256]{3,2,1,0:T(8,128)(2,1)S(1)}, bf16[2,4,32,256]{3,2,1,0:T(8,128)(2,1)S(1)}, u32[]{:S(2)}, u32[]{:S(2)}) collective-permute-start(bf16[2,4,32,256]{3,2,1,0:T(8,128)(2,1)S(1)} %slice.130), channel_id=1, source_target_pairs={{0,16},{4,20},{8,24},{12,28},{16,0},{20,4},{24,8},{28,12},{1,17},{... | collective-permute-start | bytes 393224 | tf_op jit(solution)/shard_map/ppermute | solution.py:44
  93.8 16.1 %collective-permute-start.9 = (bf16[2,4,64,256]{3,2,1,0:T(8,128)(2,1)S(1)}, bf16[2,4,64,256]{3,2,1,0:T(8,128)(2,1)S(1)}, u32[]{:S(2)}, u32[]{:S(2)}) collective-permute-start(bf16[2,4,64,256]{3,2,1,0:T(8,128)(2,1)S(1)} %slice.125), channel_id=1, source_target_pairs={{0,8},{4,12},{8,0},{12,4},{16,24},{20,28},{24,16},{28,20},{1,9},{5... | collective-permute-start | bytes 786440 | tf_op jit(solution)/shard_map/ppermute | solution.py:44
  94.4 18.8 %collective-permute-start.17 = (bf16[2,4,32,128]{3,2,1,0:T(8,128)(2,1)S(1)}, bf16[2,4,32,128]{3,2,1,0:T(8,128)(2,1)S(1)}, u32[]{:S(2)}, u32[]{:S(2)}) collective-permute-start(bf16[2,4,32,128]{3,2,1,0:T(8,128)(2,1)S(1)} %slice.134), channel_id=1, source_target_pairs={{0,16},{4,20},{8,24},{12,28},{16,0},{20,4},{24,8},{28,12},{1,17},{... | collective-permute-start | bytes 196616 | tf_op jit(solution)/shard_map/ppermute | solution.py:44
  97.0 15.0 %collective-permute-start.13 = (bf16[2,4,64,128]{3,2,1,0:T(8,128)(2,1)S(1)}, bf16[2,4,64,128]{3,2,1,0:T(8,128)(2,1)S(1)}, u32[]{:S(2)}, u32[]{:S(2)}) collective-permute-start(bf16[2,4,64,128]{3,2,1,0:T(8,128)(2,1)S(1)} %slice.129), channel_id=1, source_target_pairs={{0,8},{4,12},{8,0},{12,4},{16,24},{20,28},{24,16},{28,20},{1,9},{5... | collective-permute-start | bytes 393224 | tf_op jit(solution)/shard_map/ppermute | solution.py:44
  110.0 8.4 %collective-permute-start.16 = (bf16[2,4,32,256]{3,2,1,0:T(8,128)(2,1)S(1)}, bf16[2,4,32,256]{3,2,1,0:T(8,128)(2,1)S(1)}, u32[]{:S(2)}, u32[]{:S(2)}) collective-permute-start(bf16[2,4,32,256]{3,2,1,0:T(8,128)(2,1)S(1)} %slice.128), channel_id=1, source_target_pairs={{0,16},{4,20},{8,24},{12,28},{16,0},{20,4},{24,8},{28,12},{1,17},{... | collective-permute-start | bytes 393224 | tf_op jit(solution)/shard_map/ppermute | solution.py:44
  112.1 7.0 %collective-permute-start.18 = (bf16[2,4,32,128]{3,2,1,0:T(8,128)(2,1)S(1)}, bf16[2,4,32,128]{3,2,1,0:T(8,128)(2,1)S(1)}, u32[]{:S(2)}, u32[]{:S(2)}) collective-permute-start(bf16[2,4,32,128]{3,2,1,0:T(8,128)(2,1)S(1)} %slice.133), channel_id=1, source_target_pairs={{0,16},{4,20},{8,24},{12,28},{16,0},{20,4},{24,8},{28,12},{1,17},{... | collective-permute-start | bytes 196616 | tf_op jit(solution)/shard_map/ppermute | solution.py:44
  121.6 5.7 %collective-permute-start.21 = (f32[2,64,128]{2,1,0:T(8,128)S(1)}, f32[2,64,128]{2,1,0:T(8,128)S(1)}, u32[]{:S(2)}, u32[]{:S(2)}) collective-permute-start(f32[2,64,128]{2,1,0:T(8,128)S(1)} %get-tuple-element.79.refs_0_), channel_id=1, source_target_pairs={{0,3},{1,2},{2,1},{3,0},{4,7},{5,6},{6,5},{7,4},{8,11},{9,10},{10,... | collective-permute-start | bytes 196616 | tf_op jit(solution)/shard_map/ppermute | solution.py:44
  124.2 4.3 %collective-permute-start.20 = (f32[2,64,128]{2,1,0:T(8,128)S(1)}, f32[2,64,128]{2,1,0:T(8,128)S(1)}, u32[]{:S(2)}, u32[]{:S(2)}) collective-permute-start(f32[2,64,128]{2,1,0:T(8,128)S(1)} %get-tuple-element.79.refs_0_), channel_id=1, source_target_pairs={{0,2},{1,3},{2,0},{3,1},{4,6},{5,7},{6,4},{7,5},{8,10},{9,11},{10,... | collective-permute-start | bytes 196616 | tf_op jit(solution)/shard_map/ppermute | solution.py:44
  124.7 4.3 %collective-permute-start.19 = (f32[2,64,128]{2,1,0:T(8,128)S(1)}, f32[2,64,128]{2,1,0:T(8,128)S(1)}, u32[]{:S(2)}, u32[]{:S(2)}) collective-permute-start(f32[2,64,128]{2,1,0:T(8,128)S(1)} %get-tuple-element.79.refs_0_), channel_id=1, source_target_pairs={{0,1},{1,0},{2,3},{3,2},{4,5},{5,4},{6,7},{7,6},{8,9},{9,8},{10,11... | collective-permute-start | bytes 196616 | tf_op jit(solution)/shard_map/ppermute | solution.py:44
